TPU v7x, 8 devices: a whole 2x2x1 slice. The times are simulated.
8 devices in a mesh: dp: 1 (over z), tp: 8 (over y, x, core).
Axes of the slice: x: 2, y: 2, z: 1, core: 2. Of those that a mesh axis runs over, the one named last changes fastest.
Arguments:
- tok_hidden: bfloat16 [16, 4096], P('dp')
- seq_lens: int32 [16], P('dp')
- k_cache: bfloat16 [16, 512, 8, 128], P('dp', None, 'tp')
- v_cache: bfloat16 [16, 512, 8, 128], P('dp', None, 'tp')
- next_tok: int32 [16], P('dp')
- g_attn: bfloat16 [4096], replicated
- w_q: bfloat16 [4096, 4096], P(None, 'tp')
- b_q: bfloat16 [4096], P('tp')
- w_k: bfloat16 [4096, 1024], P(None, 'tp')
- b_k: bfloat16 [1024], P('tp')
- w_v: bfloat16 [4096, 1024], P(None, 'tp')
- b_v: bfloat16 [1024], P('tp')
- w_o: bfloat16 [4096, 4096], P('tp')
- g_mlp: bfloat16 [4096], replicated
- w_gate: bfloat16 [4096, 14336], P(None, 'tp')
- w_up: bfloat16 [4096, 14336], P(None, 'tp')
- w_down: bfloat16 [14336, 4096], P('tp')
- g_final: bfloat16 [4096], replicated
- w_head: bfloat16 [128256, 4096], P('tp')
Outputs:
- output 1: bfloat16 [16, 4096], P('dp')
- output 2: bfloat16 [16, 512, 8, 128], P('dp', None, 'tp')
- output 3: bfloat16 [16, 512, 8, 128], P('dp', None, 'tp')
- output 4: float32 [16], P('dp')
- output 5: float32 [16], P('dp')
All inputs are finite; a program needn't handle non-finite values.
Results may differ from a plain program's by a relative error of at most 0.0134601.
Values are sent between devices in bfloat16 or wider.
A program may use at most 1 GiB of HBM per device.

v0:
```python
import jax
import jax.numpy as jnp
from jax import lax
from jax.sharding import PartitionSpec as P

THETA = 1000000.0
EPS = 1e-6


def rms_norm(values, gain_vec):
    vals_f32 = values.astype(jnp.float32)
    inv_rms = lax.rsqrt(jnp.mean(vals_f32 * vals_f32, axis=-1, keepdims=True) + EPS)
    return (vals_f32 * inv_rms * gain_vec.astype(jnp.float32)).astype(jnp.bfloat16)


def rotary(values, positions):
    half_dim = values.shape[-1] // 2
    inv_freq = jnp.power(THETA, jnp.arange(half_dim, dtype=jnp.float32) * (-2.0 / values.shape[-1]))
    angles = positions.astype(jnp.float32)[:, None] * inv_freq[None, :]
    cos_part = jnp.cos(angles)[:, None, :]
    sin_part = jnp.sin(angles)[:, None, :]
    first_half = values[..., :half_dim]
    second_half = values[..., half_dim:]
    return jnp.concatenate([first_half * cos_part - second_half * sin_part, second_half * cos_part + first_half * sin_part], axis=-1)


def attention_block(tok_hidden, seq_lens, k_cache, v_cache, g_attn, w_q, b_q, w_k, b_k, w_v, b_v):
    num_rows = tok_hidden.shape[0]
    cache_len = k_cache.shape[1]
    slot_count = k_cache.shape[2]
    head_dim = k_cache.shape[3]
    head_count = w_q.shape[1] // head_dim
    group_size = head_count // slot_count
    normed = rms_norm(tok_hidden, g_attn)
    q_proj = jnp.dot(normed, w_q, preferred_element_type=jnp.float32) + b_q.astype(jnp.float32)
    k_proj = jnp.dot(normed, w_k, preferred_element_type=jnp.float32) + b_k.astype(jnp.float32)
    v_proj = jnp.dot(normed, w_v, preferred_element_type=jnp.float32) + b_v.astype(jnp.float32)
    q_rot = rotary(q_proj.reshape(num_rows, head_count, head_dim), seq_lens).astype(jnp.bfloat16)
    k_new = rotary(k_proj.reshape(num_rows, slot_count, head_dim), seq_lens).astype(jnp.bfloat16)
    v_new = v_proj.reshape(num_rows, slot_count, head_dim).astype(jnp.bfloat16)
    slot_ids = lax.broadcasted_iota(jnp.int32, (1, cache_len, 1, 1), 1)
    write_mask = slot_ids == seq_lens[:, None, None, None]
    k_all = jnp.where(write_mask, k_new[:, None], k_cache)
    v_all = jnp.where(write_mask, v_new[:, None], v_cache)
    q_grp = q_rot.reshape(num_rows, slot_count, group_size, head_dim)
    scores = jnp.einsum('bkgd,blkd->bkgl', q_grp, k_all, preferred_element_type=jnp.float32) * (head_dim ** -0.5)
    score_ids = lax.broadcasted_iota(jnp.int32, (1, 1, 1, cache_len), 3)
    scores = jnp.where(score_ids <= seq_lens[:, None, None, None], scores, -jnp.inf)
    row_max = jnp.max(scores, axis=-1, keepdims=True)
    exp_scores = jnp.exp(scores - row_max)
    attn_probs = (exp_scores / jnp.sum(exp_scores, axis=-1, keepdims=True)).astype(jnp.bfloat16)
    attn_vals = jnp.einsum('bkgl,blkd->bkgd', attn_probs, v_all, preferred_element_type=jnp.float32)
    attn_out = attn_vals.astype(jnp.bfloat16).reshape(num_rows, head_count * head_dim)
    return attn_out, k_all, v_all


def local_step(tok_hidden, seq_lens, k_cache, v_cache, next_tok, g_attn, w_q, b_q, w_k, b_k, w_v, b_v, w_o, g_mlp, w_gate, w_up, w_down, g_final, w_head):
    attn_out, k_all, v_all = attention_block(tok_hidden, seq_lens, k_cache, v_cache, g_attn, w_q, b_q, w_k, b_k, w_v, b_v)
    attn_part = jnp.dot(attn_out, w_o, preferred_element_type=jnp.float32).astype(jnp.bfloat16)
    attn_sum = lax.psum(attn_part, 'tp')
    residual = (tok_hidden.astype(jnp.float32) + attn_sum.astype(jnp.float32)).astype(jnp.bfloat16)
    mlp_in = rms_norm(residual, g_mlp)
    gate_proj = jnp.dot(mlp_in, w_gate, preferred_element_type=jnp.float32)
    up_proj = jnp.dot(mlp_in, w_up, preferred_element_type=jnp.float32)
    hidden = (jax.nn.silu(gate_proj) * up_proj).astype(jnp.bfloat16)
    down_part = jnp.dot(hidden, w_down, preferred_element_type=jnp.float32).astype(jnp.bfloat16)
    down_sum = lax.psum(down_part, 'tp')
    y_out = (residual.astype(jnp.float32) + down_sum.astype(jnp.float32)).astype(jnp.bfloat16)
    final_norm = rms_norm(y_out, g_final)
    logits = lax.dot_general(final_norm, w_head, (((1,), (1,)), ((), ())), preferred_element_type=jnp.float32)
    vocab_loc = w_head.shape[0]
    vocab_ids = lax.broadcasted_iota(jnp.int32, (1, vocab_loc), 1)
    local_tok = next_tok - lax.axis_index('tp') * vocab_loc
    local_max = jnp.max(logits, axis=1)
    local_sum = jnp.sum(jnp.exp(logits - local_max[:, None]), axis=1)
    local_target = jnp.sum(jnp.where(vocab_ids == local_tok[:, None], logits, 0.0), axis=1)
    all_stats = lax.all_gather(jnp.stack([local_max, local_sum, local_target]), 'tp')
    glob_max = jnp.max(all_stats[:, 0], axis=0)
    exp_total = jnp.sum(all_stats[:, 1] * jnp.exp(all_stats[:, 0] - glob_max[None, :]), axis=0)
    norm_lse = glob_max + jnp.log(exp_total)
    tok_logp = jnp.sum(all_stats[:, 2], axis=0) - norm_lse
    return y_out, k_all, v_all, tok_logp, norm_lse


def solution(mesh):
    row_spec = P('dp', None)
    vec_spec = P('dp')
    cache_spec = P('dp', None, 'tp', None)
    col_spec = P(None, 'tp')
    part_spec = P('tp')
    whole_spec = P(None)
    in_specs = (row_spec, vec_spec, cache_spec, cache_spec, vec_spec, whole_spec, col_spec, part_spec, col_spec, part_spec, col_spec, part_spec, P('tp', None), whole_spec, col_spec, col_spec, P('tp', None), whole_spec, P('tp', None))
    out_specs = (row_spec, cache_spec, cache_spec, vec_spec, vec_spec)
    return jax.shard_map(local_step, mesh=mesh, in_specs=in_specs, out_specs=out_specs, check_vma=False)
```

profile of v0, /device:TPU:0, one launch (start us, length us, event | category | flops | bytes accessed | tf_op | source)
XLA Modules:
  0.0 203.9 jit_solution(10500512264849970950)
XLA Ops:
  7.2 0.0 all-reduce.3.cloned.1.call-start
  7.3 0.8 convert_element_type.89
  8.1 0.7 iota_compare_fusion.2
  8.8 0.7 convert_element_type.86
  9.5 1.0 fusion.22
  10.6 0.7 convert_element_type.90
  11.2 0.1 multiply_cosine_fusion.1
  11.4 1.2 fusion.17
  12.6 0.1 fusion.59
  12.7 0.7 convert_element_type.92
  13.4 0.7 convert_element_type.88
  14.0 3.0 %convolution_add_fusion = f32[16,512]{1,0:T(8,128)S(1)} fusion(bf16[4096,512]{1,0:T(8,128)(2,1)} %param.25, f32[512]{0:T(512)S(1)} %convert_element_type.88, bf16[16,4096]{1,0:T(8,128)(2,1)} %param.19, f32[4096]{0:T(1024)S(1)} %convert_element_type.86, f32[16]{0:T(128)S(1)} %add_rsqrt_fusion.2), kind=kOutput, calls=%fused_computation.15 | convolution fusion | flops 67379200 | bytes 4376640 | tf_op jit(solution)/shard_map/dot_general | solution.py:35
  17.0 0.1 pad_maximum_fusion
  17.1 0.3 fusion.18
  17.4 0.1 subtract_convert_fusion
  17.5 4.8 %broadcast_select_fusion.1 = (bf16[16,512,1,128]{3,1,2,0:T(8,128)(2,1)S(1)}, bf16[16,512,1,128]{3,1,2,0:T(8,128)(2,1)}) fusion(bf16[16,512,1,128]{3,1,2,0:T(8,128)(2,1)} %param.21, pred[16,512]{1,0:T(8,128)(4,1)S(1)} %get-tuple-element.25, bf16[16,128]{1,0:T(8,128)(2,1)S(1)} %pad_maximum_fusion, bf16[16,512,1,128]{3,1,2,0:T(8,128)(2,1)} %param.22, ...), kind=kLoop, calls=%fused_computation.10 | loop fusion | flops 2097152 | bytes 8404992 | tf_op jit(solution)/shard_map/jit(_where)/select_n | solution.py:43
  22.3 0.7 fusion.11
  23.0 0.2 fusion.69
  23.2 2.0 fusion.14
  25.2 3.5 %convolution_convert_fusion.1 = bf16[16,4096]{1,0:T(8,128)(2,1)} fusion(bf16[512,4096]{1,0:T(8,128)(2,1)} %param.31, bf16[2,8,4,128]{3,2,1,0:T(4,128)(2,1)S(1)} %bitcast.46), kind=kOutput, calls=%fused_computation.2 | convolution fusion | flops 67174400 | bytes 4341760 | tf_op jit(solution)/shard_map/dot_general | solution.py:59
  28.7 0.0 all-reduce.3.cloned.1.call-update
  28.8 0.2 all-reduce.5.cloned.1.call-start
  29.0 44.8 %all-reduce.3.cloned.1.call-done = bf16[16,4096]{1,0:T(8,128)(2,1)} async-done(((bf16[16,4096]{1,0:T(8,128)(2,1)}), bf16[16,4096]{1,0:T(8,128)(2,1)}) %all-reduce.3.cloned.1.call-update) | async-done | bytes 131088 | tf_op jit(solution)/shard_map/psum | solution.py:60
  73.9 1.1 fusion.26
  74.9 7.2 %fusion.43 = f32[16,1792]{1,0:T(8,128)S(1)} fusion(bf16[4096,1792]{1,0:T(8,128)(2,1)} %param.33, bf16[16,4096]{1,0:T(8,128)(2,1)S(1)} %get-tuple-element.12, f32[4096]{0:T(1024)S(1)} %convert_element_type.99, f32[16]{0:T(128)S(1)} %add_rsqrt_fusion.1), kind=kOutput, calls=%fused_computation.58 | convolution fusion | flops 235143168 | bytes 14942272 | tf_op jit(solution)/shard_map/dot_general | solution.py:63
  82.2 14.4 %convolution_convert_fusion = bf16[16,4096]{1,0:T(8,128)(2,1)} fusion(bf16[1792,4096]{1,0:T(8,128)(2,1)} %param.35, bf16[4096,1792]{1,0:T(8,128)(2,1)} %param.34, f32[16,1792]{1,0:T(8,128)S(1)} %fusion.43, bf16[16,4096]{1,0:T(8,128)(2,1)S(1)} %get-tuple-element.12, f32[4096]{0:T(1024)S(1)} %convert_element_type.99, f32[16]{0:T(128)S(1)} %add_rsqrt_fusion.1), kind=kOutput, calls=%fused_computation.1 | convolution fusion | flops 470261760 | bytes 29753408 | tf_op jit(solution)/shard_map/dot_general | solution.py:66
  96.6 41.6 %all-reduce.5.cloned.1.call-done = bf16[16,4096]{1,0:T(8,128)(2,1)} async-done(((bf16[16,4096]{1,0:T(8,128)(2,1)}), bf16[16,4096]{1,0:T(8,128)(2,1)}) %all-reduce.5.cloned.1.call-update) | async-done | bytes 131088 | tf_op jit(solution)/shard_map/psum | solution.py:67
  138.2 1.1 fusion.19
  139.3 45.8 %fusion.70 = (f32[16]{0:T(128)S(1)}, f32[16,16032]{1,0:T(8,128)S(1)}) fusion(bf16[16032,4096]{1,0:T(8,128)(2,1)} %param.37, bf16[16,4096]{1,0:T(8,128)(2,1)S(1)} %get-tuple-element.10, f32[4096]{0:T(1024)S(1)} %convert_element_type.106, f32[16]{0:T(128)S(1)} %add_rsqrt_fusion), kind=kOutput, calls=%fused_computation.93 | convolution fusion | flops 2101864960 | bytes 132507776 | tf_op jit(solution)/shard_map/dot_general | solution.py:70
  185.1 0.5 exponential_reduce_fusion
  185.7 10.7 %all-gather.1 = f32[8,3,16]{2,1,0:T(4,128)S(1)} all-gather(f32[1,3,16]{2,1,0:T(4,128)S(1)} %maximum_bitcast_fusion), channel_id=2, replica_groups=mesh['dp'=1,'tp'=8] {'tp'}, dimensions={0}, use_global_device_ids=true | all-gather | bytes 1728 | tf_op jit(solution)/shard_map/all_gather | solution.py:77
  196.5 0.5 fusion.65
  (29 shorter events, 0.2 us)
Async XLA Ops:
  7.2 4.2 %copy-start = (bf16[4096,128]{1,0:T(8,128)(2,1)S(1)}, bf16[4096,128]{1,0:T(8,128)(2,1)}, u32[]{:S(2)}) copy-start(bf16[4096,128]{1,0:T(8,128)(2,1)} %param.27) | copy-start | bytes 3145732
  7.2 9.9 %copy-start.2 = (bf16[16,4096]{1,0:T(8,128)(2,1)S(1)}, bf16[16,4096]{1,0:T(8,128)(2,1)}, u32[]{:S(2)}) copy-start(bf16[16,4096]{1,0:T(8,128)(2,1)} %param.19) | copy-start | bytes 393220
  7.2 9.9 %copy-start.3 = (bf16[4096,128]{1,0:T(8,128)(2,1)S(1)}, bf16[4096,128]{1,0:T(8,128)(2,1)}, u32[]{:S(2)}) copy-start(bf16[4096,128]{1,0:T(8,128)(2,1)} %param.29) | copy-start | bytes 3145732
  7.2 66.7 %all-reduce.3.cloned.1.call-start = ((), (), s32[]{:S(2)}) async-start(), calls=%async_computation | async-start | bytes 262144 | tf_op jit(solution)/shard_map/psum | solution.py:60
  22.3 6.5 %copy-start.1 = (bf16[16,512,1,128]{3,1,2,0:T(8,128)(2,1)}, bf16[16,512,1,128]{3,1,2,0:T(8,128)(2,1)S(1)}, u32[]{:S(2)}) copy-start(bf16[16,512,1,128]{3,1,2,0:T(8,128)(2,1)S(1)} %get-tuple-element.20) | copy-start | bytes 6291460
  22.3 6.7 %copy-start.5 = (bf16[4096]{0:T(1024)(128)(2,1)S(1)}, bf16[4096]{0:T(1024)(128)(2,1)}, u32[]{:S(2)}) copy-start(bf16[4096]{0:T(1024)(128)(2,1)} %param.32) | copy-start | bytes 24580
  28.8 109.4 %all-reduce.5.cloned.1.call-start = ((), (), s32[]{:S(2)}) async-start(), calls=%async_computation.1 | async-start | bytes 262144 | tf_op jit(solution)/shard_map/psum | solution.py:67
  82.2 14.4 %copy-start.7 = (s32[16]{0:T(128)S(1)}, s32[16]{0:T(128)}, u32[]{:S(2)}) copy-start(s32[16]{0:T(128)} %param.23) | copy-start | bytes 196
  82.2 14.4 %copy-start.6 = (bf16[4096]{0:T(1024)(128)(2,1)S(1)}, bf16[4096]{0:T(1024)(128)(2,1)}, u32[]{:S(2)}) copy-start(bf16[4096]{0:T(1024)(128)(2,1)} %param.36) | copy-start | bytes 24580
  139.3 45.8 %copy-start.4 = (bf16[16,4096]{1,0:T(8,128)(2,1)}, bf16[16,4096]{1,0:T(8,128)(2,1)S(1)}, u32[]{:S(2)}) copy-start(bf16[16,4096]{1,0:T(8,128)(2,1)S(1)} %get-tuple-element.10) | copy-start | bytes 393220
Sparse Core Ops, SparseCore 0:
  28.9 44.9 all-reduce.2
  96.7 41.5 all-reduce.4
where the time goes:
time: 205 us; the launch traced here: 204 us
  waiting for transfers between devices  86.5 us (42%)
  matrix products  78.1 us (38%)
  between operations  14.2 us (7%)
  other arithmetic  14 us (7%)
  blocking collectives  10.7 us (5%)
    dot_general x1, matrix products, local_step(): lax.dot_general(final_norm, w_head, (((1,), (1,)), ((), ())), preferred_e...  45.8 us
    psum x1, waiting for transfers between devices, local_step(): attn_sum = lax.psum(attn_part, 'tp')  44.8 us
    psum x1, waiting for transfers between devices, local_step(): down_sum = lax.psum(down_part, 'tp')  41.6 us
    dot_general x1, matrix products, local_step(): jnp.dot(hidden, w_down, preferred_element_type=jnp.float32)  14.4 us
    all_gather x1, blocking collectives, local_step(): lax.all_gather(jnp.stack([local_max, local_sum, local_target]), 'tp')  10.7 us
    dot_general x1, matrix products, local_step(): gate_proj = jnp.dot(mlp_in, w_gate, preferred_element_type=jnp.float32)  7.22 us
    select_n x1, other arithmetic, attention_block(): k_all = jnp.where(write_mask, k_new[:, None], k_cache)  4.76 us
  transfers between devices with their start and end apart: 2, of which 2 were waited for; matrix products, arithmetic and copies ran while one was open for 0% of the time, Pallas kernels for 0%

commit v1 on v0

v1 whole, which is shorter than its diff:
```python
import functools

import jax
import jax.numpy as jnp
import numpy as np
from jax import lax
from jax.experimental import pallas as pl
from jax.experimental.pallas import tpu as pltpu
from jax.sharding import PartitionSpec as P

THETA = 1000000.0
EPS = 1e-6
F32 = jnp.float32
BF16 = jnp.bfloat16
ROWS = 16
D = 4096
HD = 128
GROUP = 4
LMAX = 512
FF = 1792
VOC = 16032
COL = 512
NDEV = 8
SLOTS = 14
CHUNK = 512
NFULL = VOC // CHUNK
TAIL = VOC - NFULL * CHUNK
VMEM_CAP = 64 * 2**20 - 65536

NT_DIMS = (((1,), (1,)), ((), ()))
NN_DIMS = (((1,), (0,)), ((), ()))


def mm(lhs, rhs, dims=NN_DIMS):
    return lax.dot_general(lhs, rhs, dims, preferred_element_type=F32)


def row_vector(scalars_ref, dtype, shape, axis):
    ids = lax.broadcasted_iota(jnp.int32, shape, axis)
    vec = jnp.zeros(shape, dtype)
    for row in range(ROWS):
        vec = jnp.where(ids == row, scalars_ref[row].astype(dtype), vec)
    return vec


def attn_kernel(lens_ref, x_hbm, g_ref, freq_ref, bq_ref, bk_ref, bv_ref, wq_hbm, wk_hbm, wv_hbm, kc_hbm, vc_hbm,
                ko_hbm, vo_hbm, o_ref,
                x_buf, wq, wk, wv, kbuf, vbuf, q_scr, s_scr, o_scr, sems, out_sems):
    quarter = D // 4
    bq = ROWS // 4
    copies = [pltpu.make_async_copy(x_hbm, x_buf, sems.at[0]),
              pltpu.make_async_copy(wk_hbm, wk, sems.at[1]),
              pltpu.make_async_copy(wv_hbm, wv, sems.at[2]),
              pltpu.make_async_copy(wq_hbm, wq, sems.at[3]),
              pltpu.make_async_copy(kc_hbm, kbuf, sems.at[4]),
              pltpu.make_async_copy(vc_hbm, vbuf, sems.at[5])]
    for cp in copies:
        cp.start()
    pos = row_vector(lens_ref, F32, (ROWS, HD), 0)
    angles = pos * freq_ref[...]
    cos = jnp.cos(angles)
    lane = lax.broadcasted_iota(jnp.int32, (ROWS, HD), 1)
    sin = jnp.where(lane < HD // 2, -jnp.sin(angles), jnp.sin(angles))
    copies[0].wait()
    xf = x_buf[...].astype(F32)
    inv = lax.rsqrt(jnp.mean(xf * xf, axis=-1, keepdims=True) + EPS)
    normed = (xf * inv * g_ref[...].astype(F32)).astype(BF16)
    copies[1].wait()
    k_proj = mm(normed, wk[...]) + bk_ref[...].astype(F32)
    k_new = (k_proj * cos + pltpu.roll(k_proj, HD // 2, 1) * sin).astype(BF16).astype(F32)
    copies[2].wait()
    v_new = (mm(normed, wv[...]) + bv_ref[...].astype(F32)).astype(BF16).astype(F32)
    copies[3].wait()
    q_proj = mm(normed, wq[...]) + bq_ref[...].astype(F32)
    for h in range(GROUP):
        q_h = q_proj[:, h * HD:(h + 1) * HD]
        q_scr[:, h, :] = q_h * cos + pltpu.roll(q_h, HD // 2, 1) * sin
    sub = lax.broadcasted_iota(jnp.int32, (16, HD), 0)

    def insert(buf, b, new):
        at = lens_ref[b]
        base = pl.multiple_of((at // 16) * 16, 16)
        block = buf[b, pl.ds(base, 16), :].astype(F32)
        fresh = jnp.broadcast_to(new[b:b + 1, :], (16, HD))
        buf[b, pl.ds(base, 16), :] = jnp.where(sub == at - base, fresh, block).astype(BF16)

    copies[4].wait()
    for b in range(ROWS):
        insert(kbuf, b, k_new)
    slot_ids = lax.broadcasted_iota(jnp.int32, (GROUP, LMAX), 1)
    for b in range(ROWS):
        s_b = mm(q_scr[b].astype(BF16), kbuf[b], NT_DIMS) * (HD ** -0.5)
        s_scr[b] = jnp.where(slot_ids <= lens_ref[b], s_b, -jnp.inf)
    k_out = pltpu.make_async_copy(kbuf, ko_hbm, out_sems.at[0])
    k_out.start()
    copies[5].wait()
    for b in range(ROWS):
        insert(vbuf, b, v_new)
    scores = s_scr[...]
    e = jnp.exp(scores - jnp.max(scores, axis=-1, keepdims=True))
    s_scr[...] = e / jnp.sum(e, axis=-1, keepdims=True)
    for b in range(ROWS):
        o_scr[b] = mm(s_scr[b].astype(BF16), vbuf[b])
    v_out = pltpu.make_async_copy(vbuf, vo_hbm, out_sems.at[1])
    v_out.start()
    for h in range(GROUP):
        o_ref[:, h * HD:(h + 1) * HD] = o_scr[:, h, :].astype(BF16)
    k_out.wait()
    v_out.wait()


def flip(me, k):
    out = 0
    for bit in (1, 2, 4):
        mine = lax.rem(me // bit, 2)
        out = out + bit * ((1 - mine) if k & bit else mine)
    return out


def norm_cols(parts_ref, g_ref, out_ref):
    total = jnp.zeros((ROWS, 1), F32)
    for j in range(NDEV):
        part = parts_ref[j].astype(F32)
        total = total + jnp.sum(part * part, axis=-1, keepdims=True)
    inv = lax.rsqrt(total * (1.0 / D) + EPS)
    for j in range(NDEV):
        cols = slice(j * COL, (j + 1) * COL)
        out_ref[:, cols] = (parts_ref[j].astype(F32) * inv * g_ref[:, cols].astype(F32)).astype(BF16)


def step_kernel(tok_ref, x_ref, o_ref, gm_ref, gf_ref, wo_hbm, wg_hbm, wu_hbm, wd_hbm, wh_hbm,
                y_hbm, st_ref,
                ring, mbuf, gacc, uacc, hbuf, zbuf, rs_send, rs_recv, own, gath, st_send, st_recv,
                ring_sems, rs_ssem, rs_rsem, ag_ssem, ag_rsem, st_ssem, st_rsem, y_sem):
    me = lax.axis_index('tp')
    peers = {k: flip(me, k) for k in range(1, NDEV)}
    order = (7, 6, 5, 4, 3, 2, 1)

    def fetch(c):
        slot, sem = ring.at[c % SLOTS], ring_sems.at[c % SLOTS]
        if c == 0:
            return [pltpu.make_async_copy(wo_hbm, slot, sem)]
        if c <= 8:
            rows = pl.ds((c - 1) * CHUNK, CHUNK)
            return [pltpu.make_async_copy(wg_hbm.at[rows, :], slot.at[:, 0:FF], sem),
                    pltpu.make_async_copy(wu_hbm.at[rows, :], slot.at[:, FF:2 * FF], ring_sems.at[SLOTS + c - 1])]
        first = (c - 9) * CHUNK
        size = min(CHUNK, FF - first)
        return [pltpu.make_async_copy(wd_hbm.at[pl.ds(first, size), :], slot.at[0:size, :], sem)]

    def head_copy(h, size=CHUNK):
        slot = lax.rem(h + 13, SLOTS)
        return pltpu.make_async_copy(wh_hbm.at[pl.ds(pl.multiple_of(h * CHUNK, CHUNK), size), :],
                                     ring.at[slot, 0:size, :], ring_sems.at[slot])

    for c in range(13):
        for cp in fetch(c):
            cp.start()
    head_copy(0).start()
    barrier = pltpu.get_barrier_semaphore()
    for k in order:
        pl.semaphore_signal(barrier, inc=1, device_id={'tp': peers[k]}, device_id_type=pl.DeviceIdType.MESH)
    pl.semaphore_wait(barrier, NDEV - 1)

    def remote(src, dst, ssem, rsem, k):
        return pltpu.make_async_remote_copy(src_ref=src, dst_ref=dst, send_sem=ssem, recv_sem=rsem,
                                            device_id={'tp': peers[k]}, device_id_type=pl.DeviceIdType.MESH)

    sends = []

    def all_reduce(phase, partial, residual):
        copies = {}
        for k in order:
            rs_send[phase, k] = partial(peers[k]).astype(BF16)
            copies[k] = remote(rs_send.at[phase, k], rs_recv.at[phase, k], rs_ssem.at[phase, k], rs_rsem.at[phase, k], k)
            copies[k].start()
            sends.append(copies[k])
        total = partial(me)
        for k in reversed(order):
            copies[k].wait_recv()
            total = total + rs_recv[phase, k].astype(F32)
        mine = (residual.astype(F32) + total).astype(BF16)
        own[phase] = mine
        gath[phase, me] = mine
        copies = {}
        for k in order:
            copies[k] = remote(own.at[phase], gath.at[phase, me], ag_ssem.at[phase, k], ag_rsem.at[phase, k], k)
            copies[k].start()
            sends.append(copies[k])
        for k in reversed(order):
            copies[k].wait_recv()

    def columns(dev):
        return pl.ds(pl.multiple_of(dev * COL, COL), COL)

    fetch(0)[0].wait()
    all_reduce(0, lambda dev: mm(o_ref[...], ring[0, :, columns(dev)]), x_ref[:, columns(me)])
    head_copy(1).start()
    norm_cols(gath.at[0], gm_ref, mbuf)

    for j in range(8):
        for cp in fetch(1 + j):
            cp.wait()
        m_j = mbuf[:, j * CHUNK:(j + 1) * CHUNK]
        g_j = mm(m_j, ring[1 + j, :, 0:FF])
        u_j = mm(m_j, ring[1 + j, :, FF:2 * FF])
        if j == 0:
            gacc[...] = g_j
            uacc[...] = u_j
        else:
            gacc[...] += g_j
            uacc[...] += u_j
        head_copy(2 + j).start()
    gate = gacc[...]
    hbuf[...] = (gate * jax.nn.sigmoid(gate) * uacc[...]).astype(BF16)

    for c in range(9, 13):
        fetch(c)[0].wait()

    def down(dev):
        total = jnp.zeros((ROWS, COL), F32)
        for j in range(4):
            first, size = j * CHUNK, min(CHUNK, FF - j * CHUNK)
            total = total + mm(hbuf[:, first:first + size], ring[9 + j, 0:size, columns(dev)])
        return total

    all_reduce(1, down, own[0])
    for h in range(10, 14):
        head_copy(h).start()
    y_copies = [pltpu.make_async_copy(gath.at[1, j], y_hbm.at[:, j * COL:(j + 1) * COL], y_sem.at[j]) for j in range(NDEV)]
    for cp in y_copies:
        cp.start()
    norm_cols(gath.at[1], gf_ref, mbuf)

    target = row_vector(tok_ref, jnp.int32, (1, ROWS), 1) - me * VOC

    def stats(z, first, carry):
        top, acc, hit = carry
        ids = lax.broadcasted_iota(jnp.int32, z.shape, 0) + first
        new_top = jnp.maximum(top, jnp.max(z, axis=0, keepdims=True))
        acc = acc * jnp.exp(top - new_top) + jnp.sum(jnp.exp(z - new_top), axis=0, keepdims=True)
        hit = hit + jnp.sum(jnp.where(ids == target, z, 0.0), axis=0, keepdims=True)
        return new_top, acc, hit

    def score(h, size=CHUNK):
        return mm(ring[lax.rem(h + 13, SLOTS), 0:size, :], mbuf[...], NT_DIMS)

    def refill(h):
        @pl.when(h + SLOTS < NFULL)
        def _():
            head_copy(h + SLOTS).start()

        @pl.when(h + SLOTS == NFULL)
        def _():
            head_copy(NFULL, TAIL).start()

    carry = (jnp.full((1, ROWS), -jnp.inf, F32), jnp.zeros((1, ROWS), F32), jnp.zeros((1, ROWS), F32))

    def pair(i, carry, first):
        h = 2 * i
        head_copy(h).wait()
        head_copy(h + 1).wait()
        now = lax.rem(i, 2)
        z0 = score(h)
        z1 = score(h + 1)
        if not first:
            carry = stats(zbuf[1 - now], (h - 2) * CHUNK, carry)
        zbuf[now, 0:CHUNK, :] = z0
        zbuf[now, CHUNK:, :] = z1
        refill(h)
        refill(h + 1)
        return carry

    pairs = NFULL // 2
    carry = pair(0, carry, True)
    carry = lax.fori_loop(1, pairs, lambda i, c: pair(i, c, False), carry)
    head_copy(NFULL - 1).wait()
    z_last = score(NFULL - 1)
    carry = stats(zbuf[(pairs - 1) % 2], (pairs - 1) * 2 * CHUNK, carry)
    carry = stats(z_last, (NFULL - 1) * CHUNK, carry)
    head_copy(NFULL, TAIL).wait()
    carry = stats(score(NFULL, TAIL), NFULL * CHUNK, carry)

    top, acc, hit = carry
    st_send[0:1, 0:ROWS] = top
    st_send[1:2, 0:ROWS] = acc
    st_send[2:3, 0:ROWS] = hit
    copies = {}
    for k in order:
        copies[k] = remote(st_send, st_recv.at[k], st_ssem.at[k], st_rsem.at[k], k)
        copies[k].start()
        sends.append(copies[k])
    for k in reversed(order):
        copies[k].wait_recv()
    tops, accs, hits = [top], [acc], [hit]
    for k in reversed(order):
        tops.append(st_recv[k, 0:1, 0:ROWS])
        accs.append(st_recv[k, 1:2, 0:ROWS])
        hits.append(st_recv[k, 2:3, 0:ROWS])
    best = functools.reduce(jnp.maximum, tops)
    exp_sum = sum(a * jnp.exp(t - best) for t, a in zip(tops, accs))
    lse = best + jnp.log(exp_sum)
    st_ref[0:1, 0:ROWS] = sum(hits) - lse
    st_ref[1:2, 0:ROWS] = lse
    for cp in sends:
        cp.wait_send()
    for cp in y_copies:
        cp.wait()


def rotary_freqs():
    half = HD // 2
    freq = np.power(THETA, np.arange(half) * (-2.0 / HD)).astype(np.float32)
    return np.concatenate([freq, freq])[None, :]


VM = pl.BlockSpec(memory_space=pltpu.VMEM)
SM = pl.BlockSpec(memory_space=pltpu.SMEM)
HB = pl.BlockSpec(memory_space=pl.ANY)
DMA = pltpu.SemaphoreType.DMA


def local_step(tok_hidden, seq_lens, k_cache, v_cache, next_tok, g_attn, w_q, b_q, w_k, b_k, w_v, b_v, w_o, g_mlp, w_gate, w_up, w_down, g_final, w_head):
    cache = jax.ShapeDtypeStruct((ROWS, LMAX, HD), BF16)
    k_out, v_out, attn_out = pl.pallas_call(
        attn_kernel,
        out_shape=(cache, cache, jax.ShapeDtypeStruct((ROWS, GROUP * HD), BF16)),
        in_specs=[SM, HB, VM, VM, VM, VM, VM, HB, HB, HB, HB, HB],
        out_specs=(HB, HB, VM),
        scratch_shapes=[
            pltpu.VMEM((ROWS, D), BF16),
            pltpu.VMEM((D, GROUP * HD), BF16),
            pltpu.VMEM((D, HD), BF16),
            pltpu.VMEM((D, HD), BF16),
            pltpu.VMEM((ROWS, LMAX, HD), BF16),
            pltpu.VMEM((ROWS, LMAX, HD), BF16),
            pltpu.VMEM((ROWS, GROUP, HD), F32),
            pltpu.VMEM((ROWS, GROUP, LMAX), F32),
            pltpu.VMEM((ROWS, GROUP, HD), F32),
            DMA((6,)),
            DMA((2,)),
        ],
        compiler_params=pltpu.CompilerParams(vmem_limit_bytes=48 * 2**20),
        name='attn',
    )(seq_lens, tok_hidden, g_attn[None], jnp.asarray(rotary_freqs()), b_q[None], b_k[None], b_v[None], w_q, w_k, w_v,
      k_cache.reshape(ROWS, LMAX, HD), v_cache.reshape(ROWS, LMAX, HD))
    y_out, stats = pl.pallas_call(
        step_kernel,
        out_shape=(jax.ShapeDtypeStruct((ROWS, D), BF16), jax.ShapeDtypeStruct((8, 128), F32)),
        in_specs=[SM, VM, VM, VM, VM, HB, HB, HB, HB, HB],
        out_specs=(HB, VM),
        scratch_shapes=[
            pltpu.VMEM((SLOTS, CHUNK, D), BF16),
            pltpu.VMEM((ROWS, D), BF16),
            pltpu.VMEM((ROWS, FF), F32),
            pltpu.VMEM((ROWS, FF), F32),
            pltpu.VMEM((ROWS, FF), BF16),
            pltpu.VMEM((2, 2 * CHUNK, ROWS), F32),
            pltpu.VMEM((2, NDEV, ROWS, COL), BF16),
            pltpu.VMEM((2, NDEV, ROWS, COL), BF16),
            pltpu.VMEM((2, ROWS, COL), BF16),
            pltpu.VMEM((2, NDEV, ROWS, COL), BF16),
            pltpu.VMEM((8, 128), F32),
            pltpu.VMEM((NDEV, 8, 128), F32),
            DMA((SLOTS + 8,)),
            DMA((2, NDEV)),
            DMA((2, NDEV)),
            DMA((2, NDEV)),
            DMA((2, NDEV)),
            DMA((NDEV,)),
            DMA((NDEV,)),
            DMA((NDEV,)),
        ],
        compiler_params=pltpu.CompilerParams(collective_id=0, has_side_effects=True, vmem_limit_bytes=VMEM_CAP),
        name='step',
    )(next_tok, tok_hidden, attn_out, g_mlp[None], g_final[None], w_o, w_gate, w_up, w_down, w_head)
    shape = (ROWS, LMAX, 1, HD)
    return y_out, k_out.reshape(shape), v_out.reshape(shape), stats[0, 0:ROWS], stats[1, 0:ROWS]


def solution(mesh):
    row_spec = P('dp', None)
    vec_spec = P('dp')
    cache_spec = P('dp', None, 'tp', None)
    col_spec = P(None, 'tp')
    part_spec = P('tp')
    whole_spec = P(None)
    in_specs = (row_spec, vec_spec, cache_spec, cache_spec, vec_spec, whole_spec, col_spec, part_spec, col_spec, part_spec, col_spec, part_spec, P('tp', None), whole_spec, col_spec, col_spec, P('tp', None), whole_spec, P('tp', None))
    out_specs = (row_spec, cache_spec, cache_spec, vec_spec, vec_spec)
    return jax.shard_map(local_step, mesh=mesh, in_specs=in_specs, out_specs=out_specs, check_vma=False)
```

time: 205 us -> 91.1 us (0.44)
  waiting for transfers between devices: 86.5 us -> 0 us
  matrix products: 78.1 us -> 0 us
  Pallas kernels: 0 us -> 76.5 us
  other arithmetic: 14 us -> 0 us
  local copies, waits for them, and re-layouts: 0.06 us -> 13.6 us
  between operations: 14.2 us -> 0.67 us
  blocking collectives: 10.7 us -> 0 us
    psum x2 -> x0, waiting for transfers between devices: 86.5 us -> none  [the longest x1 44.8 us: local_step(): attn_sum = lax.psum(attn_part, 'tp')]
    dot_general x9 -> x0, matrix products: 78.1 us -> none  [the longest x1 45.8 us: local_step(): lax.dot_general(final_norm, w_head, (((1,), (1,)), ((), ())), preferred_e...]
    pallas_call x0 -> x2, Pallas kernels: none -> 76.5 us  [the longest x1 70.4 us: local_step(): pl.pallas_call(step_kernel, out_shape=(jax.ShapeDtypeStruct((ROWS, D), BF...]
    all_gather x1 -> x0, blocking collectives: 10.7 us -> none  [local_step(): lax.all_gather(jnp.stack([local_max, local_sum, local_target]), 'tp')]
    unnamed x16 -> x23, local copies, waits for them, and re-layouts: 0.04 us -> 9.74 us
    select_n x1 -> x0, other arithmetic: 4.76 us -> none  [attention_block(): k_all = jnp.where(write_mask, k_new[:, None], k_cache)]
    reduce_sum x5 -> x0, other arithmetic: 3.73 us -> none  [the longest x3 3.17 us: rms_norm(): jnp.mean(vals_f32 * vals_f32, axis=-1, keepdims=True) + EPS]
    convert_element_type x7 -> x0, other arithmetic: 3.52 us -> none  [the longest x1 0.8 us: rotary(): angles = positions.astype(jnp.float32)[:, None] * inv_freq[None, :]]
  transfers between devices with their start and end apart: 2 -> 0, of which waited for: 2 -> 0; matrix products, arithmetic and copies ran while one was open for 0% -> 0% of each run, Pallas kernels for 0% -> 0%
where the time goes in v1:
time: 91.1 us; the launch traced here: 90.7 us
  Pallas kernels  76.5 us (84%)
  local copies, waits for them, and re-layouts  13.6 us (15%)
    pallas_call x1, Pallas kernels, local_step(): pl.pallas_call(step_kernel, out_shape=(jax.ShapeDtypeStruct((ROWS, D), BF...  70.4 us
    unnamed x23, local copies, waits for them, and re-layouts  9.74 us
    pallas_call x1, Pallas kernels, local_step(): pl.pallas_call(attn_kernel, out_shape=(cache, cache, jax.ShapeDtypeStruct...  6.07 us

profile of v1, /device:TPU:0, one launch (start us, length us, event | category | flops | bytes accessed | tf_op | source)
XLA Modules:
  0.0 90.7 jit_solution(4979826845965746340)
XLA Ops:
  0.6 0.7 broadcast_in_dim.18.g_ref
  1.3 0.7 broadcast_in_dim.19.bq_ref
  2.0 0.0 copy-start
  2.0 1.6 %copy-done = bf16[16,512,1,128]{3,1,2,0:T(8,128)(2,1)S(1)} copy-done((bf16[16,512,1,128]{3,1,2,0:T(8,128)(2,1)S(1)}, bf16[16,512,1,128]{3,1,2,0:T(8,128)(2,1)}, u32[]{:S(2)}) %copy-start) | copy-done | bytes 2097176
  3.6 0.0 copy-start.1
  3.6 1.2 %copy-done.1 = bf16[4096,128]{1,0:T(8,128)(2,1)S(1)} copy-done((bf16[4096,128]{1,0:T(8,128)(2,1)S(1)}, bf16[4096,128]{1,0:T(8,128)(2,1)}, u32[]{:S(2)}) %copy-start.1) | copy-done | bytes 1048600
  4.8 0.0 copy-start.2
  4.8 1.2 %copy-done.2 = bf16[4096,128]{1,0:T(8,128)(2,1)S(1)} copy-done((bf16[4096,128]{1,0:T(8,128)(2,1)S(1)}, bf16[4096,128]{1,0:T(8,128)(2,1)}, u32[]{:S(2)}) %copy-start.2) | copy-done | bytes 1048600
  6.1 0.0 copy-start.3
  6.1 0.9 copy-done.3
  7.0 0.0 copy-start.5
  7.0 0.7 copy-done.5
  7.6 0.0 copy-start.6
  7.6 0.7 copy-done.6
  8.3 0.0 copy-start.7
  8.3 0.7 copy-done.7
  8.9 0.0 copy-start.8
  8.9 0.7 copy-done.8
  9.6 0.0 copy-start.9
  9.6 0.0 copy-start.10
  9.6 6.1 %attn.1 = (bf16[16,512,128]{2,1,0:T(8,128)(2,1)}, bf16[16,512,128]{2,1,0:T(8,128)(2,1)}, bf16[16,512]{1,0:T(8,128)(2,1)S(1)}) custom-call(s32[16]{0:T(128)S(1)} %copy-done.5, bf16[16,4096]{1,0:T(8,128)(2,1)S(1)} %copy-done.3, bf16[1,4096]{1,0:T(2,128)(2,1)S(1)} %broadcast_in_dim.18.g_ref, f32[1,128]{1,0:T(1,128)S(1)} %copy-done.8, ...), custom_call_target="tpu_custom_call" | custom-call | tf_op jit(solution)/shard_map/attn/pallas_call | solution.py:325
  15.7 0.0 copy-start.4
  15.7 0.6 copy-done.4
  16.3 0.0 copy-done.9
  16.3 0.6 broadcast_in_dim.22.gm_ref
  16.9 0.0 copy-done.10
  16.9 0.6 broadcast_in_dim.23.gf_ref
  17.5 70.4 %step.1 = (bf16[16,4096]{1,0:T(8,128)(2,1)}, f32[8,128]{1,0:T(8,128)}) custom-call(s32[16]{0:T(128)} %tok_ref.1, bf16[16,4096]{1,0:T(8,128)(2,1)} %x_ref.1, bf16[16,512]{1,0:T(8,128)(2,1)} %copy-done.4, bf16[1,4096]{1,0:T(2,128)(2,1)} %broadcast_in_dim.22.gm_ref, bf16[1,4096]{1,0:T(2,128)(2,1)} %broadcast_in_dim.23.gf_ref, bf16[512,4096]{1,0:T(8,128)(2,1)} %wo_hbm.1, ...), custom_call_target="tpu_custom_call" | custom-call | tf_op jit(solution)/shard_map/step/pallas_call | solution.py:347
  87.9 1.3 %slice_bitcast_fusion = (f32[16]{0:T(128)}, f32[16]{0:T(128)}) fusion(f32[8,128]{1,0:T(8,128)} %get-tuple-element.14), kind=kLoop, calls=%fused_computation | loop fusion | bytes 256 | tf_op jit(solution)/shard_map/squeeze | solution.py:378
  89.2 1.6 %copy.28 = bf16[16,4096]{1,0:T(8,128)(2,1)} copy(bf16[16,4096]{1,0:T(8,128)(2,1)} %get-tuple-element.27) | data formatting | bytes 262144
Async XLA Ops:
  2.0 1.6 %copy-start = (bf16[16,512,1,128]{3,1,2,0:T(8,128)(2,1)S(1)}, bf16[16,512,1,128]{3,1,2,0:T(8,128)(2,1)}, u32[]{:S(2)}) copy-start(bf16[16,512,1,128]{3,1,2,0:T(8,128)(2,1)} %param.22) | copy-start | bytes 6291460
  3.6 1.2 %copy-start.1 = (bf16[4096,128]{1,0:T(8,128)(2,1)S(1)}, bf16[4096,128]{1,0:T(8,128)(2,1)}, u32[]{:S(2)}) copy-start(bf16[4096,128]{1,0:T(8,128)(2,1)} %wk_hbm.1) | copy-start | bytes 3145732
  4.8 1.2 %copy-start.2 = (bf16[4096,128]{1,0:T(8,128)(2,1)S(1)}, bf16[4096,128]{1,0:T(8,128)(2,1)}, u32[]{:S(2)}) copy-start(bf16[4096,128]{1,0:T(8,128)(2,1)} %wv_hbm.1) | copy-start | bytes 3145732
  6.1 0.9 copy-start.3
  7.0 0.7 copy-start.5
  7.6 0.7 copy-start.6
  8.3 0.7 copy-start.7
  8.9 0.7 copy-start.8
  9.6 6.7 %copy-start.9 = (bf16[4096]{0:T(1024)(128)(2,1)S(1)}, bf16[4096]{0:T(1024)(128)(2,1)}, u32[]{:S(2)}) copy-start(bf16[4096]{0:T(1024)(128)(2,1)} %param.33) | copy-start | bytes 24580
  9.6 7.3 %copy-start.10 = (bf16[4096]{0:T(1024)(128)(2,1)S(1)}, bf16[4096]{0:T(1024)(128)(2,1)}, u32[]{:S(2)}) copy-start(bf16[4096]{0:T(1024)(128)(2,1)} %param.37) | copy-start | bytes 24580
  15.7 0.6 copy-start.4

commit v2 on v1

v2 whole, which is shorter than its diff:
```python
import functools

import jax
import jax.numpy as jnp
import numpy as np
from jax import lax
from jax.experimental import pallas as pl
from jax.experimental.pallas import tpu as pltpu
from jax.sharding import PartitionSpec as P

THETA = 1000000.0
EPS = 1e-6
F32 = jnp.float32
BF16 = jnp.bfloat16
ROWS = 16
D = 4096
HD = 128
GROUP = 4
LMAX = 512
FF = 1792
VOC = 16032
COL = 512
NDEV = 8
SLOTS = 11
CHUNK = 512
DEEP = 256
HEAD0 = 13
NFULL = VOC // CHUNK
TAIL = VOC - NFULL * CHUNK
PARTS = 4
VMEM_CAP = 64 * 2**20 - 65536

NT_DIMS = (((1,), (1,)), ((), ()))
NN_DIMS = (((1,), (0,)), ((), ()))


def mm(lhs, rhs, dims=NN_DIMS):
    return lax.dot_general(lhs, rhs, dims, preferred_element_type=F32)


def row_vector(scalars_ref, dtype, shape, axis):
    ids = lax.broadcasted_iota(jnp.int32, shape, axis)
    vec = jnp.zeros(shape, dtype)
    for row in range(ROWS):
        vec = jnp.where(ids == row, scalars_ref[row].astype(dtype), vec)
    return vec


def flip(me, k):
    out = 0
    for bit in (1, 2, 4):
        mine = lax.rem(me // bit, 2)
        out = out + bit * ((1 - mine) if k & bit else mine)
    return out


def norm_cols(parts_ref, gain, out_ref):
    total = jnp.zeros((ROWS, 1), F32)
    for j in range(NDEV):
        part = parts_ref[j].astype(F32)
        total = total + jnp.sum(part * part, axis=-1, keepdims=True)
    inv = lax.rsqrt(total * (1.0 / D) + EPS)
    for j in range(NDEV):
        cols = slice(j * COL, (j + 1) * COL)
        out_ref[:, cols] = (parts_ref[j].astype(F32) * inv * gain[:, cols]).astype(BF16)


def step_kernel(lens_ref, tok_ref, x_hbm, ga_hbm, gm_ref, gf_ref, freq_ref, bq_ref, bk_ref, bv_ref,
                wq_hbm, wk_hbm, wv_hbm, kc_hbm, vc_hbm, wo_hbm, wg_hbm, wu_hbm, wd_hbm, wh_hbm,
                y_hbm, kn_ref, vn_ref, st_ref,
                ring, x_buf, ga_buf, wq, wkv, kbuf, vbuf, q_scr, s_scr, o_scr, obuf,
                mbuf, gacc, uacc, hbuf, za_buf, zb_buf, rs_send, rs_recv, own, gath, st_send, st_recv,
                in_sems, ring_sems, rs_ssem, rs_rsem, ag_ssem, ag_rsem, st_ssem, st_rsem, y_sem):
    me = lax.axis_index('tp')
    peers = {k: flip(me, k) for k in range(1, NDEV)}
    order = (7, 6, 5, 4, 3, 2, 1)

    def fetch(c):
        slot, sem = ring.at[c % SLOTS], ring_sems.at[c % SLOTS]
        if c == 0:
            return [pltpu.make_async_copy(wo_hbm, slot, sem)]
        if c <= 8:
            rows = pl.ds((c - 1) * CHUNK, CHUNK)
            return [pltpu.make_async_copy(wg_hbm.at[rows, :], slot.at[:, 0:FF], sem),
                    pltpu.make_async_copy(wu_hbm.at[rows, :], slot.at[:, FF:2 * FF], ring_sems.at[SLOTS + c - 1])]
        first = (c - 9) * CHUNK
        size = min(CHUNK, FF - first)
        return [pltpu.make_async_copy(wd_hbm.at[pl.ds(first, size), :], slot.at[0:size, :], sem)]

    def head_slot(h):
        return lax.rem(h + HEAD0, SLOTS)

    def head_copy(h, size=CHUNK):
        slot = head_slot(h)
        return pltpu.make_async_copy(wh_hbm.at[pl.ds(pl.multiple_of(h * CHUNK, CHUNK), size), :],
                                     ring.at[slot, 0:size, :], ring_sems.at[slot])

    def start_chunk(c):
        for cp in (fetch(c) if c < HEAD0 else [head_copy(c - HEAD0)]):
            cp.start()

    x_copy = pltpu.make_async_copy(x_hbm, x_buf, in_sems.at[0])
    ga_copy = pltpu.make_async_copy(ga_hbm, ga_buf, in_sems.at[1])
    wk_copy = pltpu.make_async_copy(wk_hbm, wkv.at[:, 0:HD], in_sems.at[2])
    wv_copy = pltpu.make_async_copy(wv_hbm, wkv.at[:, HD:2 * HD], in_sems.at[3])
    wq_copy = pltpu.make_async_copy(wq_hbm, wq, in_sems.at[4])
    kc_copy = pltpu.make_async_copy(kc_hbm, kbuf, in_sems.at[5])
    vc_copy = pltpu.make_async_copy(vc_hbm, vbuf, in_sems.at[6])
    for cp in (x_copy, ga_copy, wq_copy, wk_copy, wv_copy, kc_copy, vc_copy):
        cp.start()
    for c in range(SLOTS):
        start_chunk(c)
    barrier = pltpu.get_barrier_semaphore()
    for k in order:
        pl.semaphore_signal(barrier, inc=1, device_id={'tp': peers[k]}, device_id_type=pl.DeviceIdType.MESH)

    angles = row_vector(lens_ref, F32, (ROWS, HD), 0) * freq_ref[...]
    cos = jnp.cos(angles)
    lane = lax.broadcasted_iota(jnp.int32, (ROWS, HD), 1)
    sin = jnp.sin(angles)
    sin = jnp.where(lane < HD // 2, -sin, sin)
    x_copy.wait()
    ga_copy.wait()
    xf = x_buf[...].astype(F32)
    inv = lax.rsqrt(jnp.mean(xf * xf, axis=-1, keepdims=True) + EPS)
    normed = (xf * inv * ga_buf[...].astype(F32)[None, :]).astype(BF16)
    wq_copy.wait()
    q_proj = mm(normed, wq[...]) + bq_ref[...].astype(F32)[None, :]
    for h in range(GROUP):
        q_h = q_proj[:, h * HD:(h + 1) * HD]
        q_scr[:, h, :] = (q_h * cos + pltpu.roll(q_h, HD // 2, 1) * sin).astype(BF16).astype(F32)
    wk_copy.wait()
    wv_copy.wait()
    kv_proj = mm(normed, wkv[...])
    k_proj = kv_proj[:, 0:HD] + bk_ref[...].astype(F32)[None, :]
    k_new = (k_proj * cos + pltpu.roll(k_proj, HD // 2, 1) * sin).astype(BF16)
    v_new = (kv_proj[:, HD:] + bv_ref[...].astype(F32)[None, :]).astype(BF16)
    kn_ref[...] = k_new
    vn_ref[...] = v_new

    kc_copy.wait()
    slot_ids = lax.broadcasted_iota(jnp.int32, (GROUP, LMAX), 1)
    for b in range(ROWS):
        s_b = mm(q_scr[b].astype(BF16), kbuf[b], NT_DIMS) * (HD ** -0.5)
        s_scr[b] = jnp.where(slot_ids < lens_ref[b], s_b, -jnp.inf)
    s_new = jnp.sum(q_scr[...] * k_new.astype(F32)[:, None, :], axis=-1, keepdims=True) * (HD ** -0.5)
    scores = s_scr[...]
    top = jnp.maximum(jnp.max(scores, axis=-1, keepdims=True), s_new)
    e = jnp.exp(scores - top)
    e_new = jnp.exp(s_new - top)
    denom = jnp.sum(e, axis=-1, keepdims=True) + e_new
    s_scr[...] = e / denom
    p_new = (e_new / denom).astype(BF16).astype(F32)
    vc_copy.wait()
    for b in range(ROWS):
        o_scr[b] = mm(s_scr[b].astype(BF16), vbuf[b])
    o_scr[...] += p_new * v_new.astype(F32)[:, None, :]
    for h in range(GROUP):
        obuf[:, h * HD:(h + 1) * HD] = o_scr[:, h, :].astype(BF16)

    pl.semaphore_wait(barrier, NDEV - 1)

    def remote(src, dst, ssem, rsem, k):
        return pltpu.make_async_remote_copy(src_ref=src, dst_ref=dst, send_sem=ssem, recv_sem=rsem,
                                            device_id={'tp': peers[k]}, device_id_type=pl.DeviceIdType.MESH)

    sends = []

    def all_reduce(phase, partial, residual):
        copies = {}
        for k in order:
            rs_send[phase, k] = partial(peers[k]).astype(BF16)
            copies[k] = remote(rs_send.at[phase, k], rs_recv.at[phase, k], rs_ssem.at[phase, k], rs_rsem.at[phase, k], k)
            copies[k].start()
            sends.append(copies[k])
        total = partial(me)
        for k in reversed(order):
            copies[k].wait_recv()
            total = total + rs_recv[phase, k].astype(F32)
        mine = (residual.astype(F32) + total).astype(BF16)
        own[phase] = mine
        gath[phase, me] = mine
        copies = {}
        for k in order:
            copies[k] = remote(own.at[phase], gath.at[phase, me], ag_ssem.at[phase, k], ag_rsem.at[phase, k], k)
            copies[k].start()
            sends.append(copies[k])
        for k in reversed(order):
            copies[k].wait_recv()

    def columns(dev):
        return pl.ds(pl.multiple_of(dev * COL, COL), COL)

    fetch(0)[0].wait()
    all_reduce(0, lambda dev: mm(obuf[...], ring[0, :, columns(dev)]), x_buf[:, columns(me)])
    start_chunk(SLOTS)
    norm_cols(gath.at[0], gm_ref[...].astype(F32)[None, :], mbuf)

    for j in range(8):
        for cp in fetch(1 + j):
            cp.wait()
        m_j = mbuf[:, j * CHUNK:(j + 1) * CHUNK]
        g_j = mm(m_j, ring[1 + j, :, 0:FF])
        u_j = mm(m_j, ring[1 + j, :, FF:2 * FF])
        if j == 0:
            gacc[...] = g_j
            uacc[...] = u_j
        else:
            gacc[...] += g_j
            uacc[...] += u_j
        start_chunk(1 + j + SLOTS)
    gate = gacc[...]
    hbuf[...] = (gate * jax.nn.sigmoid(gate) * uacc[...]).astype(BF16)

    for c in range(9, 13):
        fetch(c)[0].wait()

    def down(dev):
        total = jnp.zeros((ROWS, COL), F32)
        for j in range(4):
            first, size = j * CHUNK, min(CHUNK, FF - j * CHUNK)
            total = total + mm(hbuf[:, first:first + size], ring[(9 + j) % SLOTS, 0:size, columns(dev)])
        return total

    all_reduce(1, down, own[0])
    for c in range(9, 13):
        start_chunk(c + SLOTS)
    y_copies = [pltpu.make_async_copy(gath.at[1, j], y_hbm.at[:, j * COL:(j + 1) * COL], y_sem.at[j]) for j in range(NDEV)]
    for cp in y_copies:
        cp.start()
    norm_cols(gath.at[1], gf_ref[...].astype(F32)[None, :], mbuf)

    target_row = row_vector(tok_ref, jnp.int32, (1, ROWS), 1) - me * VOC
    target_col = row_vector(tok_ref, jnp.int32, (ROWS, 1), 0) - me * VOC

    def fold(carry, pieces, ids, target):
        top, acc, hit = carry
        new_top = functools.reduce(jnp.maximum, pieces, top)
        acc = acc * jnp.exp(top - new_top)
        for piece, at in zip(pieces, ids):
            acc = acc + jnp.exp(piece - new_top)
            hit = hit + jnp.where(at == target, piece, 0.0)
        return new_top, acc, hit

    def stats_a(z, first, carry):
        ids = lax.broadcasted_iota(jnp.int32, (ROWS, HD), 1) + first
        n = z.shape[1] // HD
        return fold(carry, [z[:, i * HD:(i + 1) * HD] for i in range(n)], [ids + i * HD for i in range(n)], target_col)

    def stats_b(z, first, carry):
        ids = lax.broadcasted_iota(jnp.int32, (8, ROWS), 0) + first
        n = z.shape[0] // 8
        top, acc, hit = carry
        groups = z.reshape(n, 8, ROWS)
        new_top = jnp.maximum(top, jnp.max(groups, axis=0))
        acc = acc * jnp.exp(top - new_top) + jnp.sum(jnp.exp(groups - new_top[None]), axis=0)
        at = lax.broadcasted_iota(jnp.int32, (n, 8, ROWS), 0) * 8 + ids[None]
        hit = hit + jnp.sum(jnp.where(at == target_row[None], groups, 0.0), axis=0)
        return new_top, acc, hit

    def score(ha, hb, size_b):
        sa, sb = head_slot(ha), head_slot(hb)
        za = jnp.zeros((ROWS, CHUNK), F32)
        zb = jnp.zeros((size_b, ROWS), F32)
        for k in range(0, D, DEEP):
            f_k = mbuf[:, k:k + DEEP]
            za = za + mm(f_k, ring[sa, :, k:k + DEEP], NT_DIMS)
            zb = zb + mm(ring[sb, 0:size_b, k:k + DEEP], f_k, NT_DIMS)
        return za, zb

    def refill(h):
        @pl.when(h + SLOTS < NFULL)
        def _():
            head_copy(h + SLOTS).start()

        @pl.when(h + SLOTS == NFULL)
        def _():
            head_copy(NFULL, TAIL).start()

    def empty(shape):
        return jnp.full(shape, -jnp.inf, F32), jnp.zeros(shape, F32), jnp.zeros(shape, F32)

    def pair(i, carry, first):
        h = 2 * i
        head_copy(h).wait()
        head_copy(h + 1).wait()
        now = lax.rem(i, 2)
        za, zb = score(h, h + 1, CHUNK)
        if not first:
            ca, cb = carry
            ca = stats_a(za_buf[1 - now], (h - 2) * CHUNK, ca)
            cb = stats_b(zb_buf[1 - now], (h - 1) * CHUNK, cb)
            carry = (ca, cb)
        za_buf[now] = za
        zb_buf[now] = zb
        refill(h)
        refill(h + 1)
        return carry

    pairs = NFULL // 2
    carry = pair(0, (empty((ROWS, HD)), empty((8, ROWS))), True)
    carry = lax.fori_loop(1, pairs, lambda i, c: pair(i, c, False), carry)
    head_copy(NFULL - 1).wait()
    head_copy(NFULL, TAIL).wait()
    za, zb = score(NFULL - 1, NFULL, TAIL)
    ca, cb = carry
    ca = stats_a(za_buf[(pairs - 1) % 2], (2 * pairs - 2) * CHUNK, ca)
    cb = stats_b(zb_buf[(pairs - 1) % 2], (2 * pairs - 1) * CHUNK, cb)
    ca = stats_a(za, (NFULL - 1) * CHUNK, ca)
    cb = stats_b(zb, NFULL * CHUNK, cb)

    eye = lax.broadcasted_iota(jnp.int32, (ROWS, ROWS), 0) == lax.broadcasted_iota(jnp.int32, (ROWS, ROWS), 1)

    def as_row(col):
        return jnp.sum(jnp.where(eye, jnp.broadcast_to(col, (ROWS, ROWS)), 0.0), axis=0, keepdims=True)

    top_a = jnp.max(ca[0], axis=1, keepdims=True)
    acc_a = as_row(jnp.sum(ca[1] * jnp.exp(ca[0] - top_a), axis=1, keepdims=True))
    hit_a = as_row(jnp.sum(ca[2], axis=1, keepdims=True))
    top_a = as_row(top_a)
    top_b = jnp.max(cb[0], axis=0, keepdims=True)
    acc_b = jnp.sum(cb[1] * jnp.exp(cb[0] - top_b), axis=0, keepdims=True)
    hit_b = jnp.sum(cb[2], axis=0, keepdims=True)
    top = jnp.maximum(top_a, top_b)
    acc = acc_a * jnp.exp(top_a - top) + acc_b * jnp.exp(top_b - top)
    hit = hit_a + hit_b
    st_send[0:1, 0:ROWS] = top
    st_send[1:2, 0:ROWS] = acc
    st_send[2:3, 0:ROWS] = hit
    copies = {}
    for k in order:
        copies[k] = remote(st_send, st_recv.at[k], st_ssem.at[k], st_rsem.at[k], k)
        copies[k].start()
        sends.append(copies[k])
    tops, accs, hits = [top], [acc], [hit]
    for k in reversed(order):
        copies[k].wait_recv()
        tops.append(st_recv[k, 0:1, 0:ROWS])
        accs.append(st_recv[k, 1:2, 0:ROWS])
        hits.append(st_recv[k, 2:3, 0:ROWS])
    best = functools.reduce(jnp.maximum, tops)
    exp_sum = sum(a * jnp.exp(t - best) for t, a in zip(tops, accs))
    lse = best + jnp.log(exp_sum)
    st_ref[0:1, 0:ROWS] = sum(hits) - lse
    st_ref[1:2, 0:ROWS] = lse
    for cp in sends:
        cp.wait_send()
    for cp in y_copies:
        cp.wait()


def finish_kernel(lens_ref, y_hbm, kn_ref, vn_ref, st_ref, kc_hbm, vc_hbm,
                  yo_hbm, ko_hbm, vo_hbm, logp_ref, lse_ref,
                  y_buf, kbuf, vbuf, in_sems, out_sems, y_sems):
    rows = ROWS // PARTS
    y_in = pltpu.make_async_copy(y_hbm, y_buf, y_sems.at[0])
    y_in.start()

    def part(src, dst, sems, i):
        return pltpu.make_async_copy(src.at[pl.ds(i * rows, rows)], dst.at[pl.ds(i * rows, rows)], sems.at[i])

    groups = []
    for i in range(PARTS):
        for idx, (src, buf, dst, new) in enumerate(((kc_hbm, kbuf, ko_hbm, kn_ref), (vc_hbm, vbuf, vo_hbm, vn_ref))):
            copy = part(src, buf, in_sems.at[idx], i)
            copy.start()
            groups.append((i, buf, new, copy, part(buf, dst, out_sems.at[idx], i)))
    logp_ref[...] = st_ref[0, 0:ROWS]
    lse_ref[...] = st_ref[1, 0:ROWS]
    sub = lax.broadcasted_iota(jnp.int32, (16, HD), 0)
    y_in.wait()
    y_out = pltpu.make_async_copy(y_buf, yo_hbm, y_sems.at[1])
    y_out.start()
    for i, buf, new, copy, out in groups:
        copy.wait()
        fresh = new[...].astype(F32)
        for b in range(i * rows, (i + 1) * rows):
            at = lens_ref[b]
            base = pl.multiple_of((at // 16) * 16, 16)
            block = buf[b, pl.ds(base, 16), :].astype(F32)
            row = jnp.broadcast_to(fresh[b:b + 1, :], (16, HD))
            buf[b, pl.ds(base, 16), :] = jnp.where(sub == at - base, row, block).astype(BF16)
        out.start()
    y_out.wait()
    for *_, out in groups:
        out.wait()


def rotary_freqs():
    half = HD // 2
    freq = np.power(THETA, np.arange(half) * (-2.0 / HD)).astype(np.float32)
    return np.concatenate([freq, freq])[None, :]


VM = pl.BlockSpec(memory_space=pltpu.VMEM)
SM = pl.BlockSpec(memory_space=pltpu.SMEM)
HB = pl.BlockSpec(memory_space=pl.ANY)
DMA = pltpu.SemaphoreType.DMA


def local_step(tok_hidden, seq_lens, k_cache, v_cache, next_tok, g_attn, w_q, b_q, w_k, b_k, w_v, b_v, w_o, g_mlp, w_gate, w_up, w_down, g_final, w_head):
    k_cache = k_cache.reshape(ROWS, LMAX, HD)
    v_cache = v_cache.reshape(ROWS, LMAX, HD)
    hidden = jax.ShapeDtypeStruct((ROWS, D), BF16)
    new_row = jax.ShapeDtypeStruct((ROWS, HD), BF16)
    cache = jax.ShapeDtypeStruct((ROWS, LMAX, HD), BF16)
    vector = jax.ShapeDtypeStruct((ROWS,), F32)
    y, k_new, v_new, stats = pl.pallas_call(
        step_kernel,
        out_shape=(hidden, new_row, new_row, jax.ShapeDtypeStruct((8, 128), F32)),
        in_specs=[SM, SM, HB, HB, VM, VM, VM, VM, VM, VM] + [HB] * 10,
        out_specs=(HB, VM, VM, VM),
        scratch_shapes=[
            pltpu.VMEM((SLOTS, CHUNK, D), BF16),
            pltpu.VMEM((ROWS, D), BF16),
            pltpu.VMEM((D,), BF16),
            pltpu.VMEM((D, GROUP * HD), BF16),
            pltpu.VMEM((D, 2 * HD), BF16),
            pltpu.VMEM((ROWS, LMAX, HD), BF16),
            pltpu.VMEM((ROWS, LMAX, HD), BF16),
            pltpu.VMEM((ROWS, GROUP, HD), F32),
            pltpu.VMEM((ROWS, GROUP, LMAX), F32),
            pltpu.VMEM((ROWS, GROUP, HD), F32),
            pltpu.VMEM((ROWS, GROUP * HD), BF16),
            pltpu.VMEM((ROWS, D), BF16),
            pltpu.VMEM((ROWS, FF), F32),
            pltpu.VMEM((ROWS, FF), F32),
            pltpu.VMEM((ROWS, FF), BF16),
            pltpu.VMEM((2, ROWS, CHUNK), F32),
            pltpu.VMEM((2, CHUNK, ROWS), F32),
            pltpu.VMEM((2, NDEV, ROWS, COL), BF16),
            pltpu.VMEM((2, NDEV, ROWS, COL), BF16),
            pltpu.VMEM((2, ROWS, COL), BF16),
            pltpu.VMEM((2, NDEV, ROWS, COL), BF16),
            pltpu.VMEM((8, 128), F32),
            pltpu.VMEM((NDEV, 8, 128), F32),
            DMA((7,)),
            DMA((SLOTS + 8,)),
            DMA((2, NDEV)),
            DMA((2, NDEV)),
            DMA((2, NDEV)),
            DMA((2, NDEV)),
            DMA((NDEV,)),
            DMA((NDEV,)),
            DMA((NDEV,)),
        ],
        compiler_params=pltpu.CompilerParams(collective_id=0, has_side_effects=True, vmem_limit_bytes=VMEM_CAP),
        name='step',
    )(seq_lens, next_tok, tok_hidden, g_attn, g_mlp, g_final, jnp.asarray(rotary_freqs()), b_q, b_k, b_v,
      w_q, w_k, w_v, k_cache, v_cache, w_o, w_gate, w_up, w_down, w_head)
    y_out, k_out, v_out, logp, lse = pl.pallas_call(
        finish_kernel,
        out_shape=(hidden, cache, cache, vector, vector),
        in_specs=[SM, HB, VM, VM, VM, HB, HB],
        out_specs=(HB, HB, HB, VM, VM),
        scratch_shapes=[
            pltpu.VMEM((ROWS, D), BF16),
            pltpu.VMEM((ROWS, LMAX, HD), BF16),
            pltpu.VMEM((ROWS, LMAX, HD), BF16),
            DMA((2, PARTS)),
            DMA((2, PARTS)),
            DMA((2,)),
        ],
        compiler_params=pltpu.CompilerParams(vmem_limit_bytes=VMEM_CAP),
        name='finish',
    )(seq_lens, y, k_new, v_new, stats, k_cache, v_cache)
    shape = (ROWS, LMAX, 1, HD)
    return y_out, k_out.reshape(shape), v_out.reshape(shape), logp, lse


def solution(mesh):
    row_spec = P('dp', None)
    vec_spec = P('dp')
    cache_spec = P('dp', None, 'tp', None)
    col_spec = P(None, 'tp')
    part_spec = P('tp')
    whole_spec = P(None)
    in_specs = (row_spec, vec_spec, cache_spec, cache_spec, vec_spec, whole_spec, col_spec, part_spec, col_spec, part_spec, col_spec, part_spec, P('tp', None), whole_spec, col_spec, col_spec, P('tp', None), whole_spec, P('tp', None))
    out_specs = (row_spec, cache_spec, cache_spec, vec_spec, vec_spec)
    return jax.shard_map(local_step, mesh=mesh, in_specs=in_specs, out_specs=out_specs, check_vma=False)
```

time: 91.1 us -> 81.8 us (0.90)
  local copies, waits for them, and re-layouts: 13.6 us -> 0 us
  Pallas kernels: 76.5 us -> 80.8 us
    unnamed x23 -> x0, local copies, waits for them, and re-layouts: 9.74 us -> none
    pallas_call x2, Pallas kernels: 76.5 us -> 80.8 us  [the longest x1 75.2 us: local_step(): pl.pallas_call(step_kernel, out_shape=(hidden, new_row, new_row, jax.Shap...]
    broadcast_in_dim x4 -> x0, local copies, waits for them, and re-layouts: 2.61 us -> none  [the longest x1 0.71 us: local_step(): g_attn[None]]
    squeeze x1 -> x0, local copies, waits for them, and re-layouts: 1.27 us -> none  [local_step(): stats[1, 0:ROWS]]
where the time goes in v2:
time: 81.8 us; the launch traced here: 81.6 us
  Pallas kernels  80.8 us (99%)
    pallas_call x1, Pallas kernels, local_step(): pl.pallas_call(step_kernel, out_shape=(hidden, new_row, new_row, jax.Shap...  75.2 us
    pallas_call x1, Pallas kernels, local_step(): pl.pallas_call(finish_kernel, out_shape=(hidden, cache, cache, vector, ve...  5.52 us

profile of v2, /device:TPU:0, one launch (start us, length us, event | category | flops | bytes accessed | tf_op | source)
XLA Modules:
  0.0 81.6 jit_solution(8928560014271811072)
XLA Ops:
  0.6 75.2 %step.1 = (bf16[16,4096]{1,0:T(8,128)(2,1)}, bf16[16,128]{1,0:T(8,128)(2,1)}, bf16[16,128]{1,0:T(8,128)(2,1)}, f32[8,128]{1,0:T(8,128)}) custom-call(s32[16]{0:T(128)} %lens_ref.3, s32[16]{0:T(128)} %tok_ref.1, bf16[16,4096]{1,0:T(8,128)(2,1)} %x_hbm.1, bf16[4096]{0:T(1024)(128)(2,1)} %ga_hbm.1, bf16[4096]{0:T(1024)(128)(2,1)} %gm_ref.1, ...), custom_call_target="tpu_custom_call" | custom-call | tf_op jit(solution)/shard_map/step/pallas_call | solution.py:408
  75.9 5.5 %finish.1 = (bf16[16,4096]{1,0:T(8,128)(2,1)}, bf16[16,512,128]{2,1,0:T(8,128)(2,1)}, bf16[16,512,128]{2,1,0:T(8,128)(2,1)}, f32[16]{0:T(128)}, f32[16]{0:T(128)}) custom-call(s32[16]{0:T(128)} %lens_ref.3, bf16[16,4096]{1,0:T(8,128)(2,1)} %get-tuple-element.14.y_hbm, bf16[16,128]{1,0:T(8,128)(2,1)} %get-tuple-element.15.kn_ref, ...), custom_call_target="tpu_custom_call" | custom-call | tf_op jit(solution)/shard_map/finish/pallas_call | solution.py:451

commit v3 on v2

--- a/solution.py
+++ b/solution.py
@@ -21,12 +21,17 @@
 VOC = 16032
 COL = 512
 NDEV = 8
-SLOTS = 11
+SLOTS = 14
 CHUNK = 512
 DEEP = 256
-HEAD0 = 13
+WO = 3
+GU0 = 4
+DN0 = 12
+HEAD0 = 16
 NFULL = VOC // CHUNK
-TAIL = VOC - NFULL * CHUNK
+REST = VOC - NFULL * CHUNK
+PAIRS = NFULL // 2
+QUARTERS = 4
 PARTS = 4
 VMEM_CAP = 64 * 2**20 - 65536
 
@@ -65,48 +70,72 @@
         out_ref[:, cols] = (parts_ref[j].astype(F32) * inv * gain[:, cols]).astype(BF16)
 
 
-def step_kernel(lens_ref, tok_ref, x_hbm, ga_hbm, gm_ref, gf_ref, freq_ref, bq_ref, bk_ref, bv_ref,
+def step_kernel(lens_hbm, tok_hbm, x_hbm, ga_hbm, gm_hbm, gf_hbm, freq_hbm, bq_hbm, bk_hbm, bv_hbm,
                 wq_hbm, wk_hbm, wv_hbm, kc_hbm, vc_hbm, wo_hbm, wg_hbm, wu_hbm, wd_hbm, wh_hbm,
-                y_hbm, kn_ref, vn_ref, st_ref,
-                ring, x_buf, ga_buf, wq, wkv, kbuf, vbuf, q_scr, s_scr, o_scr, obuf,
+                y_hbm, kn_hbm, vn_hbm, st_ref,
+                ring, lens_ref, tok_ref, x_buf, ga_ref, gm_ref, gf_ref, freq_ref, bq_ref, bk_ref, bv_ref,
+                kn_buf, vn_buf, q_scr, s_scr, o_scr, obuf,
                 mbuf, gacc, uacc, hbuf, za_buf, zb_buf, rs_send, rs_recv, own, gath, st_send, st_recv,
-                in_sems, ring_sems, rs_ssem, rs_rsem, ag_ssem, ag_rsem, st_ssem, st_rsem, y_sem):
+                small_sems, wq_sems, wkv_sems, cache_sems, ring_sems, last_sems,
+                rs_ssem, rs_rsem, ag_ssem, ag_rsem, st_ssem, st_rsem, out_sems):
     me = lax.axis_index('tp')
     peers = {k: flip(me, k) for k in range(1, NDEV)}
     order = (7, 6, 5, 4, 3, 2, 1)
+    copy = pltpu.make_async_copy
 
     def fetch(c):
         slot, sem = ring.at[c % SLOTS], ring_sems.at[c % SLOTS]
+        blocks = [pl.ds(j * CHUNK, CHUNK) for j in range(D // CHUNK)]
         if c == 0:
-            return [pltpu.make_async_copy(wo_hbm, slot, sem)]
-        if c <= 8:
-            rows = pl.ds((c - 1) * CHUNK, CHUNK)
-            return [pltpu.make_async_copy(wg_hbm.at[rows, :], slot.at[:, 0:FF], sem),
-                    pltpu.make_async_copy(wu_hbm.at[rows, :], slot.at[:, FF:2 * FF], ring_sems.at[SLOTS + c - 1])]
-        first = (c - 9) * CHUNK
+            return [copy(wq_hbm.at[rows, :], slot.at[:, j * COL:(j + 1) * COL], wq_sems.at[j]) for j, rows in enumerate(blocks)]
+        if c == 1:
+            return [copy(src.at[rows, :], slot.at[:, (2 * j + i) * HD:(2 * j + i + 1) * HD], wkv_sems.at[2 * j + i])
+                    for j, rows in enumerate(blocks) for i, src in enumerate((wk_hbm, wv_hbm))]
+        if c == 2:
+            return [copy(src.at[b], slot.at[:, (i * ROWS + b) * HD:(i * ROWS + b + 1) * HD], cache_sems.at[i * ROWS + b])
+                    for i, src in enumerate((kc_hbm, vc_hbm)) for b in range(ROWS)]
+        if c == WO:
+            return [copy(wo_hbm, slot, sem)]
+        if c < DN0:
+            rows = pl.ds((c - GU0) * CHUNK, CHUNK)
+            return [copy(wg_hbm.at[rows, :], slot.at[:, 0:FF], sem),
+                    copy(wu_hbm.at[rows, :], slot.at[:, FF:2 * FF], ring_sems.at[SLOTS + c - GU0])]
+        first = (c - DN0) * CHUNK
         size = min(CHUNK, FF - first)
-        return [pltpu.make_async_copy(wd_hbm.at[pl.ds(first, size), :], slot.at[0:size, :], sem)]
+        return [copy(wd_hbm.at[pl.ds(first, size), :], slot.at[0:size, :], sem)]
 
     def head_slot(h):
         return lax.rem(h + HEAD0, SLOTS)
 
-    def head_copy(h, size=CHUNK):
+    def head_row(h):
+        return REST + (h - 1) * CHUNK
+
+    def head_rest():
+        return copy(wh_hbm.at[0:REST, :], ring.at[HEAD0 % SLOTS, 0:REST, :], ring_sems.at[HEAD0 % SLOTS])
+
+    def head_copy(h):
         slot = head_slot(h)
-        return pltpu.make_async_copy(wh_hbm.at[pl.ds(pl.multiple_of(h * CHUNK, CHUNK), size), :],
-                                     ring.at[slot, 0:size, :], ring_sems.at[slot])
+        return copy(wh_hbm.at[pl.ds(pl.multiple_of(head_row(h), 32), CHUNK), :], ring.at[slot], ring_sems.at[slot])
+
+    def head_quarters(h):
+        slot = (h + HEAD0) % SLOTS
+        size = D // QUARTERS
+        return [copy(wh_hbm.at[pl.ds(head_row(h), CHUNK), q * size:(q + 1) * size], ring.at[slot, :, q * size:(q + 1) * size],
+                     last_sems.at[(NFULL - h) * QUARTERS + q]) for q in range(QUARTERS)]
 
     def start_chunk(c):
-        for cp in (fetch(c) if c < HEAD0 else [head_copy(c - HEAD0)]):
-            cp.start()
-
-    x_copy = pltpu.make_async_copy(x_hbm, x_buf, in_sems.at[0])
-    ga_copy = pltpu.make_async_copy(ga_hbm, ga_buf, in_sems.at[1])
-    wk_copy = pltpu.make_async_copy(wk_hbm, wkv.at[:, 0:HD], in_sems.at[2])
-    wv_copy = pltpu.make_async_copy(wv_hbm, wkv.at[:, HD:2 * HD], in_sems.at[3])
-    wq_copy = pltpu.make_async_copy(wq_hbm, wq, in_sems.at[4])
-    kc_copy = pltpu.make_async_copy(kc_hbm, kbuf, in_sems.at[5])
-    vc_copy = pltpu.make_async_copy(vc_hbm, vbuf, in_sems.at[6])
-    for cp in (x_copy, ga_copy, wq_copy, wk_copy, wv_copy, kc_copy, vc_copy):
+        if c < HEAD0:
+            for cp in fetch(c):
+                cp.start(priority=0 if c < WO else 1)
+        elif c == HEAD0:
+            head_rest().start(priority=1)
+        else:
+            head_copy(c - HEAD0).start(priority=1)
+
+    smalls = [copy(src, dst, small_sems.at[i]) for i, (src, dst) in enumerate((
+        (x_hbm, x_buf), (ga_hbm, ga_ref), (lens_hbm, lens_ref), (freq_hbm, freq_ref), (bq_hbm, bq_ref), (bk_hbm, bk_ref),
+        (bv_hbm, bv_ref), (gm_hbm, gm_ref), (gf_hbm, gf_ref), (tok_hbm, tok_ref)))]
+    for cp in smalls:
         cp.start()
     for c in range(SLOTS):
         start_chunk(c)
@@ -114,34 +143,42 @@
     for k in order:
         pl.semaphore_signal(barrier, inc=1, device_id={'tp': peers[k]}, device_id_type=pl.DeviceIdType.MESH)
 
+    for cp in smalls:
+        cp.wait()
     angles = row_vector(lens_ref, F32, (ROWS, HD), 0) * freq_ref[...]
     cos = jnp.cos(angles)
     lane = lax.broadcasted_iota(jnp.int32, (ROWS, HD), 1)
     sin = jnp.sin(angles)
     sin = jnp.where(lane < HD // 2, -sin, sin)
-    x_copy.wait()
-    ga_copy.wait()
     xf = x_buf[...].astype(F32)
     inv = lax.rsqrt(jnp.mean(xf * xf, axis=-1, keepdims=True) + EPS)
-    normed = (xf * inv * ga_buf[...].astype(F32)[None, :]).astype(BF16)
-    wq_copy.wait()
-    q_proj = mm(normed, wq[...]) + bq_ref[...].astype(F32)[None, :]
+    normed = (xf * inv * ga_ref[...].astype(F32)[None, :]).astype(BF16)
+    for cp in fetch(0):
+        cp.wait()
+    q_proj = bq_ref[...].astype(F32)[None, :]
+    for j in range(D // CHUNK):
+        q_proj = q_proj + mm(normed[:, j * CHUNK:(j + 1) * CHUNK], ring[0, :, j * COL:(j + 1) * COL])
+    start_chunk(SLOTS)
     for h in range(GROUP):
         q_h = q_proj[:, h * HD:(h + 1) * HD]
         q_scr[:, h, :] = (q_h * cos + pltpu.roll(q_h, HD // 2, 1) * sin).astype(BF16).astype(F32)
-    wk_copy.wait()
-    wv_copy.wait()
-    kv_proj = mm(normed, wkv[...])
+    for cp in fetch(1):
+        cp.wait()
+    kv_proj = jnp.zeros((ROWS, 2 * HD), F32)
+    for j in range(D // CHUNK):
+        kv_proj = kv_proj + mm(normed[:, j * CHUNK:(j + 1) * CHUNK], ring[1, :, 2 * j * HD:2 * (j + 1) * HD])
+    start_chunk(1 + SLOTS)
     k_proj = kv_proj[:, 0:HD] + bk_ref[...].astype(F32)[None, :]
     k_new = (k_proj * cos + pltpu.roll(k_proj, HD // 2, 1) * sin).astype(BF16)
     v_new = (kv_proj[:, HD:] + bv_ref[...].astype(F32)[None, :]).astype(BF16)
-    kn_ref[...] = k_new
-    vn_ref[...] = v_new
-
-    kc_copy.wait()
+    kn_buf[...] = k_new
+    vn_buf[...] = v_new
+
+    for cp in fetch(2):
+        cp.wait()
     slot_ids = lax.broadcasted_iota(jnp.int32, (GROUP, LMAX), 1)
     for b in range(ROWS):
-        s_b = mm(q_scr[b].astype(BF16), kbuf[b], NT_DIMS) * (HD ** -0.5)
+        s_b = mm(q_scr[b].astype(BF16), ring[2, :, b * HD:(b + 1) * HD], NT_DIMS) * (HD ** -0.5)
         s_scr[b] = jnp.where(slot_ids < lens_ref[b], s_b, -jnp.inf)
     s_new = jnp.sum(q_scr[...] * k_new.astype(F32)[:, None, :], axis=-1, keepdims=True) * (HD ** -0.5)
     scores = s_scr[...]
@@ -151,12 +188,15 @@
     denom = jnp.sum(e, axis=-1, keepdims=True) + e_new
     s_scr[...] = e / denom
     p_new = (e_new / denom).astype(BF16).astype(F32)
-    vc_copy.wait()
     for b in range(ROWS):
-        o_scr[b] = mm(s_scr[b].astype(BF16), vbuf[b])
+        o_scr[b] = mm(s_scr[b].astype(BF16), ring[2, :, (ROWS + b) * HD:(ROWS + b + 1) * HD])
     o_scr[...] += p_new * v_new.astype(F32)[:, None, :]
     for h in range(GROUP):
         obuf[:, h * HD:(h + 1) * HD] = o_scr[:, h, :].astype(BF16)
+    start_chunk(2 + SLOTS)
+    outs = [copy(kn_buf, kn_hbm, out_sems.at[NDEV]), copy(vn_buf, vn_hbm, out_sems.at[NDEV + 1])]
+    for cp in outs:
+        cp.start()
 
     pl.semaphore_wait(barrier, NDEV - 1)
 
@@ -166,7 +206,7 @@
 
     sends = []
 
-    def all_reduce(phase, partial, residual):
+    def all_reduce(phase, partial, residual, used):
         copies = {}
         for k in order:
             rs_send[phase, k] = partial(peers[k]).astype(BF16)
@@ -174,6 +214,8 @@
             copies[k].start()
             sends.append(copies[k])
         total = partial(me)
+        for c in used:
+            start_chunk(c + SLOTS)
         for k in reversed(order):
             copies[k].wait_recv()
             total = total + rs_recv[phase, k].astype(F32)
@@ -191,43 +233,40 @@
     def columns(dev):
         return pl.ds(pl.multiple_of(dev * COL, COL), COL)
 
-    fetch(0)[0].wait()
-    all_reduce(0, lambda dev: mm(obuf[...], ring[0, :, columns(dev)]), x_buf[:, columns(me)])
-    start_chunk(SLOTS)
+    fetch(WO)[0].wait()
+    all_reduce(0, lambda dev: mm(obuf[...], ring[WO, :, columns(dev)]), x_buf[:, columns(me)], (WO,))
     norm_cols(gath.at[0], gm_ref[...].astype(F32)[None, :], mbuf)
 
     for j in range(8):
-        for cp in fetch(1 + j):
+        for cp in fetch(GU0 + j):
             cp.wait()
         m_j = mbuf[:, j * CHUNK:(j + 1) * CHUNK]
-        g_j = mm(m_j, ring[1 + j, :, 0:FF])
-        u_j = mm(m_j, ring[1 + j, :, FF:2 * FF])
+        g_j = mm(m_j, ring[(GU0 + j) % SLOTS, :, 0:FF])
+        u_j = mm(m_j, ring[(GU0 + j) % SLOTS, :, FF:2 * FF])
         if j == 0:
             gacc[...] = g_j
             uacc[...] = u_j
         else:
             gacc[...] += g_j
             uacc[...] += u_j
-        start_chunk(1 + j + SLOTS)
+        start_chunk(GU0 + j + SLOTS)
     gate = gacc[...]
     hbuf[...] = (gate * jax.nn.sigmoid(gate) * uacc[...]).astype(BF16)
 
-    for c in range(9, 13):
+    for c in range(DN0, HEAD0):
         fetch(c)[0].wait()
 
     def down(dev):
         total = jnp.zeros((ROWS, COL), F32)
         for j in range(4):
             first, size = j * CHUNK, min(CHUNK, FF - j * CHUNK)
-            total = total + mm(hbuf[:, first:first + size], ring[(9 + j) % SLOTS, 0:size, columns(dev)])
+            total = total + mm(hbuf[:, first:first + size], ring[(DN0 + j) % SLOTS, 0:size, columns(dev)])
         return total
 
-    all_reduce(1, down, own[0])
-    for c in range(9, 13):
-        start_chunk(c + SLOTS)
-    y_copies = [pltpu.make_async_copy(gath.at[1, j], y_hbm.at[:, j * COL:(j + 1) * COL], y_sem.at[j]) for j in range(NDEV)]
-    for cp in y_copies:
-        cp.start()
+    all_reduce(1, down, own[0], range(DN0, HEAD0))
+    for j in range(NDEV):
+        outs.append(copy(gath.at[1, j], y_hbm.at[:, j * COL:(j + 1) * COL], out_sems.at[j]))
+        outs[-1].start()
     norm_cols(gath.at[1], gf_ref[...].astype(F32)[None, :], mbuf)
 
     target_row = row_vector(tok_ref, jnp.int32, (1, ROWS), 1) - me * VOC
@@ -258,56 +297,80 @@
         hit = hit + jnp.sum(jnp.where(at == target_row[None], groups, 0.0), axis=0)
         return new_top, acc, hit
 
-    def score(ha, hb, size_b):
-        sa, sb = head_slot(ha), head_slot(hb)
-        za = jnp.zeros((ROWS, CHUNK), F32)
-        zb = jnp.zeros((size_b, ROWS), F32)
-        for k in range(0, D, DEEP):
+    def score(sa, sb, size_b, first, last, sums):
+        sums = list(sums)
+        for k in range(first, last, DEEP):
             f_k = mbuf[:, k:k + DEEP]
-            za = za + mm(f_k, ring[sa, :, k:k + DEEP], NT_DIMS)
-            zb = zb + mm(ring[sb, 0:size_b, k:k + DEEP], f_k, NT_DIMS)
-        return za, zb
-
-    def refill(h):
-        @pl.when(h + SLOTS < NFULL)
-        def _():
-            head_copy(h + SLOTS).start()
-
-        @pl.when(h + SLOTS == NFULL)
-        def _():
-            head_copy(NFULL, TAIL).start()
+            for i, q in enumerate(range(0, CHUNK, DEEP)):
+                sums[2 * i] = sums[2 * i] + mm(f_k, ring[sa, q:q + DEEP, k:k + DEEP], NT_DIMS)
+                if q < size_b:
+                    end = min(q + DEEP, size_b)
+                    sums[2 * i + 1] = sums[2 * i + 1] + mm(ring[sb, q:end, k:k + DEEP], f_k, NT_DIMS)
+        return sums
+
+    def zeros(size_b):
+        sums = []
+        for q in range(0, CHUNK, DEEP):
+            sums += [jnp.zeros((ROWS, DEEP), F32), jnp.zeros((min(DEEP, size_b - q), ROWS), F32) if q < size_b else None]
+        return sums
 
     def empty(shape):
         return jnp.full(shape, -jnp.inf, F32), jnp.zeros(shape, F32), jnp.zeros(shape, F32)
 
-    def pair(i, carry, first):
+    def keep(sums, now):
+        for i, q in enumerate(range(0, CHUNK, DEEP)):
+            za_buf[now, :, q:q + DEEP] = sums[2 * i]
+            zb_buf[now, q:q + DEEP, :] = sums[2 * i + 1]
+
+    def stats(now, h, carry):
+        return stats_a(za_buf[now], head_row(h), carry[0]), stats_b(zb_buf[now], head_row(h + 1), carry[1])
+
+    def refill(h):
+        @pl.when(h + SLOTS < 2 * PAIRS)
+        def _():
+            head_copy(h + SLOTS).start(priority=1)
+
+    head_rest().wait()
+    head_copy(1).wait()
+    sums = score(head_slot(1), HEAD0 % SLOTS, REST, 0, D, zeros(REST))
+    ca = stats_a(sums[0], head_row(1), empty((ROWS, HD)))
+    carry = (stats_a(sums[2], head_row(1) + DEEP, ca), stats_b(sums[1], 0, empty((8, ROWS))))
+    for h in (0, 1):
+        head_copy(h + SLOTS).start(priority=1)
+
+    def pair(i, carry, first=False):
         h = 2 * i
         head_copy(h).wait()
         head_copy(h + 1).wait()
-        now = lax.rem(i, 2)
-        za, zb = score(h, h + 1, CHUNK)
+        sums = score(head_slot(h), head_slot(h + 1), CHUNK, 0, D, zeros(CHUNK))
         if not first:
-            ca, cb = carry
-            ca = stats_a(za_buf[1 - now], (h - 2) * CHUNK, ca)
-            cb = stats_b(zb_buf[1 - now], (h - 1) * CHUNK, cb)
-            carry = (ca, cb)
-        za_buf[now] = za
-        zb_buf[now] = zb
+            carry = stats(lax.rem(i - 1, 2), h - 2, carry)
+        keep(sums, lax.rem(i, 2))
         refill(h)
         refill(h + 1)
+
+        @pl.when(h + SLOTS == 2 * PAIRS)
+        def _():
+            for q in range(QUARTERS):
+                for cp in (last_a[q], last_b[q]):
+                    cp.start(priority=1)
         return carry
 
-    pairs = NFULL // 2
-    carry = pair(0, (empty((ROWS, HD)), empty((8, ROWS))), True)
-    carry = lax.fori_loop(1, pairs, lambda i, c: pair(i, c, False), carry)
-    head_copy(NFULL - 1).wait()
-    head_copy(NFULL, TAIL).wait()
-    za, zb = score(NFULL - 1, NFULL, TAIL)
+    last_a, last_b = head_quarters(2 * PAIRS), head_quarters(2 * PAIRS + 1)
+    carry = pair(1, carry, True)
+    carry = lax.fori_loop(2, PAIRS, pair, carry)
+    sums = zeros(CHUNK)
+    size = D // QUARTERS
+    for q in range(QUARTERS):
+        last_a[q].wait()
+        last_b[q].wait()
+        sums = score((2 * PAIRS + HEAD0) % SLOTS, (2 * PAIRS + 1 + HEAD0) % SLOTS, CHUNK, q * size, (q + 1) * size, sums)
+        if q == 0:
+            carry = stats((PAIRS - 1) % 2, 2 * PAIRS - 2, carry)
     ca, cb = carry
-    ca = stats_a(za_buf[(pairs - 1) % 2], (2 * pairs - 2) * CHUNK, ca)
-    cb = stats_b(zb_buf[(pairs - 1) % 2], (2 * pairs - 1) * CHUNK, cb)
-    ca = stats_a(za, (NFULL - 1) * CHUNK, ca)
-    cb = stats_b(zb, NFULL * CHUNK, cb)
+    for i, q in enumerate(range(0, CHUNK, DEEP)):
+        ca = stats_a(sums[2 * i], head_row(2 * PAIRS) + q, ca)
+        cb = stats_b(sums[2 * i + 1], head_row(2 * PAIRS + 1) + q, cb)
 
     eye = lax.broadcasted_iota(jnp.int32, (ROWS, ROWS), 0) == lax.broadcasted_iota(jnp.int32, (ROWS, ROWS), 1)
 
@@ -345,34 +408,37 @@
     st_ref[1:2, 0:ROWS] = lse
     for cp in sends:
         cp.wait_send()
-    for cp in y_copies:
-        cp.wait()
-
-
-def finish_kernel(lens_ref, y_hbm, kn_ref, vn_ref, st_ref, kc_hbm, vc_hbm,
-                  yo_hbm, ko_hbm, vo_hbm, logp_ref, lse_ref,
-                  y_buf, kbuf, vbuf, in_sems, out_sems, y_sems):
+    for cp in outs:
+        cp.wait()
+
+
+def finish_kernel(lens_hbm, y_hbm, kn_hbm, vn_hbm, st_hbm, kc_hbm, vc_hbm,
+                  yo_hbm, ko_hbm, vo_hbm, logp_hbm, lse_hbm,
+                  lens_ref, y_buf, kn_ref, vn_ref, st_ref, logp_ref, lse_ref, kbuf, vbuf, in_sems, out_sems, small_sems):
     rows = ROWS // PARTS
-    y_in = pltpu.make_async_copy(y_hbm, y_buf, y_sems.at[0])
-    y_in.start()
+    copy = pltpu.make_async_copy
 
     def part(src, dst, sems, i):
-        return pltpu.make_async_copy(src.at[pl.ds(i * rows, rows)], dst.at[pl.ds(i * rows, rows)], sems.at[i])
-
+        return copy(src.at[pl.ds(i * rows, rows)], dst.at[pl.ds(i * rows, rows)], sems.at[i])
+
+    smalls = [copy(src, dst, small_sems.at[i]) for i, (src, dst) in enumerate((
+        (lens_hbm, lens_ref), (kn_hbm, kn_ref), (vn_hbm, vn_ref), (st_hbm, st_ref), (y_hbm, y_buf)))]
+    for cp in smalls:
+        cp.start()
     groups = []
     for i in range(PARTS):
         for idx, (src, buf, dst, new) in enumerate(((kc_hbm, kbuf, ko_hbm, kn_ref), (vc_hbm, vbuf, vo_hbm, vn_ref))):
-            copy = part(src, buf, in_sems.at[idx], i)
-            copy.start()
-            groups.append((i, buf, new, copy, part(buf, dst, out_sems.at[idx], i)))
+            fill = part(src, buf, in_sems.at[idx], i)
+            fill.start()
+            groups.append((i, buf, new, fill, part(buf, dst, out_sems.at[idx], i)))
+    sub = lax.broadcasted_iota(jnp.int32, (16, HD), 0)
+    for cp in smalls:
+        cp.wait()
     logp_ref[...] = st_ref[0, 0:ROWS]
     lse_ref[...] = st_ref[1, 0:ROWS]
-    sub = lax.broadcasted_iota(jnp.int32, (16, HD), 0)
-    y_in.wait()
-    y_out = pltpu.make_async_copy(y_buf, yo_hbm, y_sems.at[1])
-    y_out.start()
-    for i, buf, new, copy, out in groups:
-        copy.wait()
+    outs = [copy(y_buf, yo_hbm, small_sems.at[5]), copy(logp_ref, logp_hbm, small_sems.at[6]), copy(lse_ref, lse_hbm, small_sems.at[7])]
+    for i, buf, new, fill, out in groups:
+        fill.wait()
         fresh = new[...].astype(F32)
         for b in range(i * rows, (i + 1) * rows):
             at = lens_ref[b]
@@ -381,7 +447,12 @@
             row = jnp.broadcast_to(fresh[b:b + 1, :], (16, HD))
             buf[b, pl.ds(base, 16), :] = jnp.where(sub == at - base, row, block).astype(BF16)
         out.start()
-    y_out.wait()
+        if outs and i == 0:
+            for cp in outs:
+                cp.start()
+            waits, outs = outs, []
+    for cp in waits:
+        cp.wait()
     for *_, out in groups:
         out.wait()
 
@@ -393,7 +464,6 @@
 
 
 VM = pl.BlockSpec(memory_space=pltpu.VMEM)
-SM = pl.BlockSpec(memory_space=pltpu.SMEM)
 HB = pl.BlockSpec(memory_space=pl.ANY)
 DMA = pltpu.SemaphoreType.DMA
 
@@ -408,16 +478,22 @@
     y, k_new, v_new, stats = pl.pallas_call(
         step_kernel,
         out_shape=(hidden, new_row, new_row, jax.ShapeDtypeStruct((8, 128), F32)),
-        in_specs=[SM, SM, HB, HB, VM, VM, VM, VM, VM, VM] + [HB] * 10,
-        out_specs=(HB, VM, VM, VM),
+        in_specs=[HB] * 20,
+        out_specs=(HB, HB, HB, VM),
         scratch_shapes=[
             pltpu.VMEM((SLOTS, CHUNK, D), BF16),
+            pltpu.SMEM((ROWS,), jnp.int32),
+            pltpu.SMEM((ROWS,), jnp.int32),
             pltpu.VMEM((ROWS, D), BF16),
             pltpu.VMEM((D,), BF16),
-            pltpu.VMEM((D, GROUP * HD), BF16),
-            pltpu.VMEM((D, 2 * HD), BF16),
-            pltpu.VMEM((ROWS, LMAX, HD), BF16),
-            pltpu.VMEM((ROWS, LMAX, HD), BF16),
+            pltpu.VMEM((D,), BF16),
+            pltpu.VMEM((D,), BF16),
+            pltpu.VMEM((1, HD), F32),
+            pltpu.VMEM((GROUP * HD,), BF16),
+            pltpu.VMEM((HD,), BF16),
+            pltpu.VMEM((HD,), BF16),
+            pltpu.VMEM((ROWS, HD), BF16),
+            pltpu.VMEM((ROWS, HD), BF16),
             pltpu.VMEM((ROWS, GROUP, HD), F32),
             pltpu.VMEM((ROWS, GROUP, LMAX), F32),
             pltpu.VMEM((ROWS, GROUP, HD), F32),
@@ -434,15 +510,19 @@
             pltpu.VMEM((2, NDEV, ROWS, COL), BF16),
             pltpu.VMEM((8, 128), F32),
             pltpu.VMEM((NDEV, 8, 128), F32),
-            DMA((7,)),
+            DMA((10,)),
+            DMA((8,)),
+            DMA((16,)),
+            DMA((2 * ROWS,)),
             DMA((SLOTS + 8,)),
+            DMA((2 * QUARTERS,)),
             DMA((2, NDEV)),
             DMA((2, NDEV)),
             DMA((2, NDEV)),
             DMA((2, NDEV)),
             DMA((NDEV,)),
             DMA((NDEV,)),
-            DMA((NDEV,)),
+            DMA((NDEV + 2,)),
         ],
         compiler_params=pltpu.CompilerParams(collective_id=0, has_side_effects=True, vmem_limit_bytes=VMEM_CAP),
         name='step',
@@ -451,15 +531,21 @@
     y_out, k_out, v_out, logp, lse = pl.pallas_call(
         finish_kernel,
         out_shape=(hidden, cache, cache, vector, vector),
-        in_specs=[SM, HB, VM, VM, VM, HB, HB],
-        out_specs=(HB, HB, HB, VM, VM),
+        in_specs=[HB] * 7,
+        out_specs=(HB,) * 5,
         scratch_shapes=[
+            pltpu.SMEM((ROWS,), jnp.int32),
             pltpu.VMEM((ROWS, D), BF16),
+            pltpu.VMEM((ROWS, HD), BF16),
+            pltpu.VMEM((ROWS, HD), BF16),
+            pltpu.VMEM((8, 128), F32),
+            pltpu.VMEM((ROWS,), F32),
+            pltpu.VMEM((ROWS,), F32),
             pltpu.VMEM((ROWS, LMAX, HD), BF16),
             pltpu.VMEM((ROWS, LMAX, HD), BF16),
             DMA((2, PARTS)),
             DMA((2, PARTS)),
-            DMA((2,)),
+            DMA((8,)),
         ],
         compiler_params=pltpu.CompilerParams(vmem_limit_bytes=VMEM_CAP),
         name='finish',

time: 81.8 us -> 69.8 us (0.85)
  Pallas kernels: 80.8 us -> 68.9 us
    pallas_call x1, Pallas kernels: 75.2 us -> 64.6 us  [local_step(): pl.pallas_call(step_kernel, out_shape=(hidden, new_row, new_row, jax.Shap...]
    pallas_call x1, Pallas kernels: 5.52 us -> 4.29 us  [local_step(): pl.pallas_call(finish_kernel, out_shape=(hidden, cache, cache, vector, ve...]
where the time goes in v3:
time: 69.8 us; the launch traced here: 69.7 us
  Pallas kernels  68.9 us (99%)
  between operations  0.81 us (1%)
    pallas_call x1, Pallas kernels, local_step(): pl.pallas_call(step_kernel, out_shape=(hidden, new_row, new_row, jax.Shap...  64.6 us
    pallas_call x1, Pallas kernels, local_step(): pl.pallas_call(finish_kernel, out_shape=(hidden, cache, cache, vector, ve...  4.29 us

profile of v3, /device:TPU:0, one launch (start us, length us, event | category | flops | bytes accessed | tf_op | source)
XLA Modules:
  0.0 69.7 jit_solution(13290761896059111706)
XLA Ops:
  0.6 64.6 %step.1 = (bf16[16,4096]{1,0:T(8,128)(2,1)}, bf16[16,128]{1,0:T(8,128)(2,1)}, bf16[16,128]{1,0:T(8,128)(2,1)}, f32[8,128]{1,0:T(8,128)}) custom-call(s32[16]{0:T(128)} %lens_hbm.3, s32[16]{0:T(128)} %tok_hbm.1, bf16[16,4096]{1,0:T(8,128)(2,1)} %x_hbm.1, bf16[4096]{0:T(1024)(128)(2,1)} %ga_hbm.1, bf16[4096]{0:T(1024)(128)(2,1)} %gm_hbm.1, ...), custom_call_target="tpu_custom_call" | custom-call | tf_op jit(solution)/shard_map/step/pallas_call | solution.py:478
  65.3 4.3 %finish.1 = (bf16[16,4096]{1,0:T(8,128)(2,1)}, bf16[16,512,128]{2,1,0:T(8,128)(2,1)}, bf16[16,512,128]{2,1,0:T(8,128)(2,1)}, f32[16]{0:T(128)}, f32[16]{0:T(128)}) custom-call(s32[16]{0:T(128)} %lens_hbm.3, bf16[16,4096]{1,0:T(8,128)(2,1)} %get-tuple-element.14.y_hbm, bf16[16,128]{1,0:T(8,128)(2,1)} %get-tuple-element.15.kn_hbm, ...), custom_call_target="tpu_custom_call" | custom-call | tf_op jit(solution)/shard_map/finish/pallas_call | solution.py:531

commit v4 on v3

--- a/solution.py
+++ b/solution.py
@@ -21,19 +21,18 @@
 VOC = 16032
 COL = 512
 NDEV = 8
-SLOTS = 14
+SLOTS = 12
 CHUNK = 512
 DEEP = 256
-WO = 3
-GU0 = 4
-DN0 = 12
-HEAD0 = 16
+WO = 2
+GU0 = 3
+DN0 = 11
+HEAD0 = 15
 NFULL = VOC // CHUNK
 REST = VOC - NFULL * CHUNK
 PAIRS = NFULL // 2
 QUARTERS = 4
-PARTS = 4
-VMEM_CAP = 64 * 2**20 - 65536
+STEP_VMEM = 56 * 2**20
 
 NT_DIMS = (((1,), (1,)), ((), ()))
 NN_DIMS = (((1,), (0,)), ((), ()))
@@ -72,12 +71,11 @@
 
 def step_kernel(lens_hbm, tok_hbm, x_hbm, ga_hbm, gm_hbm, gf_hbm, freq_hbm, bq_hbm, bk_hbm, bv_hbm,
                 wq_hbm, wk_hbm, wv_hbm, kc_hbm, vc_hbm, wo_hbm, wg_hbm, wu_hbm, wd_hbm, wh_hbm,
-                y_hbm, kn_hbm, vn_hbm, st_ref,
+                y_ref, k_ref, v_ref, st_ref,
                 ring, lens_ref, tok_ref, x_buf, ga_ref, gm_ref, gf_ref, freq_ref, bq_ref, bk_ref, bv_ref,
-                kn_buf, vn_buf, q_scr, s_scr, o_scr, obuf,
+                q_scr, s_scr, o_scr, obuf,
                 mbuf, gacc, uacc, hbuf, za_buf, zb_buf, rs_send, rs_recv, own, gath, st_send, st_recv,
-                small_sems, wq_sems, wkv_sems, cache_sems, ring_sems, last_sems,
-                rs_ssem, rs_rsem, ag_ssem, ag_rsem, st_ssem, st_rsem, out_sems):
+                small_sems, cache_sems, ring_sems, last_sems, send_sems, recv_sems):
     me = lax.axis_index('tp')
     peers = {k: flip(me, k) for k in range(1, NDEV)}
     order = (7, 6, 5, 4, 3, 2, 1)
@@ -87,22 +85,24 @@
         slot, sem = ring.at[c % SLOTS], ring_sems.at[c % SLOTS]
         blocks = [pl.ds(j * CHUNK, CHUNK) for j in range(D // CHUNK)]
         if c == 0:
-            return [copy(wq_hbm.at[rows, :], slot.at[:, j * COL:(j + 1) * COL], wq_sems.at[j]) for j, rows in enumerate(blocks)]
+            return [copy(wq_hbm.at[rows, :], slot.at[:, j * COL:(j + 1) * COL], sem) for j, rows in enumerate(blocks)]
         if c == 1:
-            return [copy(src.at[rows, :], slot.at[:, (2 * j + i) * HD:(2 * j + i + 1) * HD], wkv_sems.at[2 * j + i])
+            return [copy(src.at[rows, :], slot.at[:, (2 * j + i) * HD:(2 * j + i + 1) * HD], sem)
                     for j, rows in enumerate(blocks) for i, src in enumerate((wk_hbm, wv_hbm))]
-        if c == 2:
-            return [copy(src.at[b], slot.at[:, (i * ROWS + b) * HD:(i * ROWS + b + 1) * HD], cache_sems.at[i * ROWS + b])
-                    for i, src in enumerate((kc_hbm, vc_hbm)) for b in range(ROWS)]
         if c == WO:
             return [copy(wo_hbm, slot, sem)]
         if c < DN0:
             rows = pl.ds((c - GU0) * CHUNK, CHUNK)
             return [copy(wg_hbm.at[rows, :], slot.at[:, 0:FF], sem),
-                    copy(wu_hbm.at[rows, :], slot.at[:, FF:2 * FF], ring_sems.at[SLOTS + c - GU0])]
+                    copy(wu_hbm.at[rows, :], slot.at[:, FF:2 * FF], sem)]
         first = (c - DN0) * CHUNK
         size = min(CHUNK, FF - first)
         return [copy(wd_hbm.at[pl.ds(first, size), :], slot.at[0:size, :], sem)]
+
+    def landed(c):
+        width = {0: D, 1: 2 * HD * (D // CHUNK)}.get(c, 2 * FF if GU0 <= c < DN0 else D)
+        rows = min(CHUNK, FF - (c - DN0) * CHUNK) if c >= DN0 else CHUNK
+        copy(wo_hbm.at[0:rows, 0:width], ring.at[c % SLOTS, 0:rows, 0:width], ring_sems.at[c % SLOTS]).wait()
 
     def head_slot(h):
         return lax.rem(h + HEAD0, SLOTS)
@@ -121,7 +121,7 @@
         slot = (h + HEAD0) % SLOTS
         size = D // QUARTERS
         return [copy(wh_hbm.at[pl.ds(head_row(h), CHUNK), q * size:(q + 1) * size], ring.at[slot, :, q * size:(q + 1) * size],
-                     last_sems.at[(NFULL - h) * QUARTERS + q]) for q in range(QUARTERS)]
+                     last_sems.at[q]) for q in range(QUARTERS)]
 
     def start_chunk(c):
         if c < HEAD0:
@@ -137,7 +137,11 @@
         (bv_hbm, bv_ref), (gm_hbm, gm_ref), (gf_hbm, gf_ref), (tok_hbm, tok_ref)))]
     for cp in smalls:
         cp.start()
+    caches = [copy(kc_hbm, k_ref, cache_sems.at[0]), copy(vc_hbm, v_ref, cache_sems.at[1])]
     for c in range(SLOTS):
+        if c == WO:
+            for cp in caches:
+                cp.start()
         start_chunk(c)
     barrier = pltpu.get_barrier_semaphore()
     for k in order:
@@ -153,8 +157,7 @@
     xf = x_buf[...].astype(F32)
     inv = lax.rsqrt(jnp.mean(xf * xf, axis=-1, keepdims=True) + EPS)
     normed = (xf * inv * ga_ref[...].astype(F32)[None, :]).astype(BF16)
-    for cp in fetch(0):
-        cp.wait()
+    landed(0)
     q_proj = bq_ref[...].astype(F32)[None, :]
     for j in range(D // CHUNK):
         q_proj = q_proj + mm(normed[:, j * CHUNK:(j + 1) * CHUNK], ring[0, :, j * COL:(j + 1) * COL])
@@ -162,8 +165,7 @@
     for h in range(GROUP):
         q_h = q_proj[:, h * HD:(h + 1) * HD]
         q_scr[:, h, :] = (q_h * cos + pltpu.roll(q_h, HD // 2, 1) * sin).astype(BF16).astype(F32)
-    for cp in fetch(1):
-        cp.wait()
+    landed(1)
     kv_proj = jnp.zeros((ROWS, 2 * HD), F32)
     for j in range(D // CHUNK):
         kv_proj = kv_proj + mm(normed[:, j * CHUNK:(j + 1) * CHUNK], ring[1, :, 2 * j * HD:2 * (j + 1) * HD])
@@ -171,14 +173,11 @@
     k_proj = kv_proj[:, 0:HD] + bk_ref[...].astype(F32)[None, :]
     k_new = (k_proj * cos + pltpu.roll(k_proj, HD // 2, 1) * sin).astype(BF16)
     v_new = (kv_proj[:, HD:] + bv_ref[...].astype(F32)[None, :]).astype(BF16)
-    kn_buf[...] = k_new
-    vn_buf[...] = v_new
-
-    for cp in fetch(2):
-        cp.wait()
+
+    caches[0].wait()
     slot_ids = lax.broadcasted_iota(jnp.int32, (GROUP, LMAX), 1)
     for b in range(ROWS):
-        s_b = mm(q_scr[b].astype(BF16), ring[2, :, b * HD:(b + 1) * HD], NT_DIMS) * (HD ** -0.5)
+        s_b = mm(q_scr[b].astype(BF16), k_ref[b], NT_DIMS) * (HD ** -0.5)
         s_scr[b] = jnp.where(slot_ids < lens_ref[b], s_b, -jnp.inf)
     s_new = jnp.sum(q_scr[...] * k_new.astype(F32)[:, None, :], axis=-1, keepdims=True) * (HD ** -0.5)
     scores = s_scr[...]
@@ -188,15 +187,12 @@
     denom = jnp.sum(e, axis=-1, keepdims=True) + e_new
     s_scr[...] = e / denom
     p_new = (e_new / denom).astype(BF16).astype(F32)
+    caches[1].wait()
     for b in range(ROWS):
-        o_scr[b] = mm(s_scr[b].astype(BF16), ring[2, :, (ROWS + b) * HD:(ROWS + b + 1) * HD])
+        o_scr[b] = mm(s_scr[b].astype(BF16), v_ref[b])
     o_scr[...] += p_new * v_new.astype(F32)[:, None, :]
     for h in range(GROUP):
         obuf[:, h * HD:(h + 1) * HD] = o_scr[:, h, :].astype(BF16)
-    start_chunk(2 + SLOTS)
-    outs = [copy(kn_buf, kn_hbm, out_sems.at[NDEV]), copy(vn_buf, vn_hbm, out_sems.at[NDEV + 1])]
-    for cp in outs:
-        cp.start()
 
     pl.semaphore_wait(barrier, NDEV - 1)
 
@@ -204,42 +200,49 @@
         return pltpu.make_async_remote_copy(src_ref=src, dst_ref=dst, send_sem=ssem, recv_sem=rsem,
                                             device_id={'tp': peers[k]}, device_id_type=pl.DeviceIdType.MESH)
 
-    sends = []
-
-    def all_reduce(phase, partial, residual, used):
-        copies = {}
+    def exchange(phase, payload, landing, size):
         for k in order:
+            remote(payload(k), landing(k), send_sems.at[phase], recv_sems.at[phase], k).start()
+        return remote(size, size, send_sems.at[phase], recv_sems.at[phase], 1)
+
+    def all_reduce(phase, partial, residual, used, meanwhile):
+        def send_part(k):
             rs_send[phase, k] = partial(peers[k]).astype(BF16)
-            copies[k] = remote(rs_send.at[phase, k], rs_recv.at[phase, k], rs_ssem.at[phase, k], rs_rsem.at[phase, k], k)
-            copies[k].start()
-            sends.append(copies[k])
+            return rs_send.at[phase, k]
+
+        seven = rs_recv.at[phase, 1:NDEV]
+        scatter = exchange(2 * phase, send_part, lambda k: rs_recv.at[phase, k], seven)
         total = partial(me)
         for c in used:
             start_chunk(c + SLOTS)
+        meanwhile()
+        scatter.wait_recv()
         for k in reversed(order):
-            copies[k].wait_recv()
             total = total + rs_recv[phase, k].astype(F32)
         mine = (residual.astype(F32) + total).astype(BF16)
         own[phase] = mine
         gath[phase, me] = mine
-        copies = {}
-        for k in order:
-            copies[k] = remote(own.at[phase], gath.at[phase, me], ag_ssem.at[phase, k], ag_rsem.at[phase, k], k)
-            copies[k].start()
-            sends.append(copies[k])
-        for k in reversed(order):
-            copies[k].wait_recv()
+        gather = exchange(2 * phase + 1, lambda k: own.at[phase], lambda k: gath.at[phase, me], seven)
+        gather.wait_recv()
+        return [scatter, gather]
 
     def columns(dev):
         return pl.ds(pl.multiple_of(dev * COL, COL), COL)
 
-    fetch(WO)[0].wait()
-    all_reduce(0, lambda dev: mm(obuf[...], ring[WO, :, columns(dev)]), x_buf[:, columns(me)], (WO,))
+    def insert():
+        ids = lax.broadcasted_iota(jnp.int32, (LMAX, HD), 0)
+        for b in range(ROWS):
+            here = ids == lens_ref[b]
+            for ref, new in ((k_ref, k_new), (v_ref, v_new)):
+                row = jnp.broadcast_to(new[b:b + 1, :].astype(F32), (LMAX, HD))
+                ref[b] = jnp.where(here, row, ref[b].astype(F32)).astype(BF16)
+
+    landed(WO)
+    sends = all_reduce(0, lambda dev: mm(obuf[...], ring[WO, :, columns(dev)]), x_buf[:, columns(me)], (WO,), insert)
     norm_cols(gath.at[0], gm_ref[...].astype(F32)[None, :], mbuf)
 
     for j in range(8):
-        for cp in fetch(GU0 + j):
-            cp.wait()
+        landed(GU0 + j)
         m_j = mbuf[:, j * CHUNK:(j + 1) * CHUNK]
         g_j = mm(m_j, ring[(GU0 + j) % SLOTS, :, 0:FF])
         u_j = mm(m_j, ring[(GU0 + j) % SLOTS, :, FF:2 * FF])
@@ -254,7 +257,7 @@
     hbuf[...] = (gate * jax.nn.sigmoid(gate) * uacc[...]).astype(BF16)
 
     for c in range(DN0, HEAD0):
-        fetch(c)[0].wait()
+        landed(c)
 
     def down(dev):
         total = jnp.zeros((ROWS, COL), F32)
@@ -263,10 +266,9 @@
             total = total + mm(hbuf[:, first:first + size], ring[(DN0 + j) % SLOTS, 0:size, columns(dev)])
         return total
 
-    all_reduce(1, down, own[0], range(DN0, HEAD0))
+    sends += all_reduce(1, down, own[0], range(DN0, HEAD0), lambda: None)
     for j in range(NDEV):
-        outs.append(copy(gath.at[1, j], y_hbm.at[:, j * COL:(j + 1) * COL], out_sems.at[j]))
-        outs[-1].start()
+        y_ref[:, j * COL:(j + 1) * COL] = gath[1, j]
     norm_cols(gath.at[1], gf_ref[...].astype(F32)[None, :], mbuf)
 
     target_row = row_vector(tok_ref, jnp.int32, (1, ROWS), 1) - me * VOC
@@ -362,8 +364,7 @@
     sums = zeros(CHUNK)
     size = D // QUARTERS
     for q in range(QUARTERS):
-        last_a[q].wait()
-        last_b[q].wait()
+        copy(wo_hbm.at[:, 0:2 * size], ring.at[0, :, 0:2 * size], last_sems.at[q]).wait()
         sums = score((2 * PAIRS + HEAD0) % SLOTS, (2 * PAIRS + 1 + HEAD0) % SLOTS, CHUNK, q * size, (q + 1) * size, sums)
         if q == 0:
             carry = stats((PAIRS - 1) % 2, 2 * PAIRS - 2, carry)
@@ -390,14 +391,10 @@
     st_send[0:1, 0:ROWS] = top
     st_send[1:2, 0:ROWS] = acc
     st_send[2:3, 0:ROWS] = hit
-    copies = {}
-    for k in order:
-        copies[k] = remote(st_send, st_recv.at[k], st_ssem.at[k], st_rsem.at[k], k)
-        copies[k].start()
-        sends.append(copies[k])
+    share = exchange(4, lambda k: st_send, lambda k: st_recv.at[k], st_recv.at[1:NDEV])
+    share.wait_recv()
     tops, accs, hits = [top], [acc], [hit]
     for k in reversed(order):
-        copies[k].wait_recv()
         tops.append(st_recv[k, 0:1, 0:ROWS])
         accs.append(st_recv[k, 1:2, 0:ROWS])
         hits.append(st_recv[k, 2:3, 0:ROWS])
@@ -406,55 +403,19 @@
     lse = best + jnp.log(exp_sum)
     st_ref[0:1, 0:ROWS] = sum(hits) - lse
     st_ref[1:2, 0:ROWS] = lse
-    for cp in sends:
-        cp.wait_send()
-    for cp in outs:
-        cp.wait()
-
-
-def finish_kernel(lens_hbm, y_hbm, kn_hbm, vn_hbm, st_hbm, kc_hbm, vc_hbm,
-                  yo_hbm, ko_hbm, vo_hbm, logp_hbm, lse_hbm,
-                  lens_ref, y_buf, kn_ref, vn_ref, st_ref, logp_ref, lse_ref, kbuf, vbuf, in_sems, out_sems, small_sems):
-    rows = ROWS // PARTS
-    copy = pltpu.make_async_copy
-
-    def part(src, dst, sems, i):
-        return copy(src.at[pl.ds(i * rows, rows)], dst.at[pl.ds(i * rows, rows)], sems.at[i])
-
-    smalls = [copy(src, dst, small_sems.at[i]) for i, (src, dst) in enumerate((
-        (lens_hbm, lens_ref), (kn_hbm, kn_ref), (vn_hbm, vn_ref), (st_hbm, st_ref), (y_hbm, y_buf)))]
-    for cp in smalls:
-        cp.start()
-    groups = []
-    for i in range(PARTS):
-        for idx, (src, buf, dst, new) in enumerate(((kc_hbm, kbuf, ko_hbm, kn_ref), (vc_hbm, vbuf, vo_hbm, vn_ref))):
-            fill = part(src, buf, in_sems.at[idx], i)
-            fill.start()
-            groups.append((i, buf, new, fill, part(buf, dst, out_sems.at[idx], i)))
-    sub = lax.broadcasted_iota(jnp.int32, (16, HD), 0)
-    for cp in smalls:
-        cp.wait()
+    for group in sends + [share]:
+        group.wait_send()
+
+
+def finish_kernel(y_ref, k_ref, v_ref, st_ref, y_hbm, k_hbm, v_hbm, logp_hbm, lse_hbm, logp_ref, lse_ref, sems):
     logp_ref[...] = st_ref[0, 0:ROWS]
     lse_ref[...] = st_ref[1, 0:ROWS]
-    outs = [copy(y_buf, yo_hbm, small_sems.at[5]), copy(logp_ref, logp_hbm, small_sems.at[6]), copy(lse_ref, lse_hbm, small_sems.at[7])]
-    for i, buf, new, fill, out in groups:
-        fill.wait()
-        fresh = new[...].astype(F32)
-        for b in range(i * rows, (i + 1) * rows):
-            at = lens_ref[b]
-            base = pl.multiple_of((at // 16) * 16, 16)
-            block = buf[b, pl.ds(base, 16), :].astype(F32)
-            row = jnp.broadcast_to(fresh[b:b + 1, :], (16, HD))
-            buf[b, pl.ds(base, 16), :] = jnp.where(sub == at - base, row, block).astype(BF16)
-        out.start()
-        if outs and i == 0:
-            for cp in outs:
-                cp.start()
-            waits, outs = outs, []
-    for cp in waits:
+    copies = [pltpu.make_async_copy(src, dst, sems.at[i]) for i, (src, dst) in enumerate((
+        (k_ref, k_hbm), (v_ref, v_hbm), (y_ref, y_hbm), (logp_ref, logp_hbm), (lse_ref, lse_hbm)))]
+    for cp in copies:
+        cp.start()
+    for cp in copies:
         cp.wait()
-    for *_, out in groups:
-        out.wait()
 
 
 def rotary_freqs():
@@ -472,14 +433,14 @@
     k_cache = k_cache.reshape(ROWS, LMAX, HD)
     v_cache = v_cache.reshape(ROWS, LMAX, HD)
     hidden = jax.ShapeDtypeStruct((ROWS, D), BF16)
-    new_row = jax.ShapeDtypeStruct((ROWS, HD), BF16)
     cache = jax.ShapeDtypeStruct((ROWS, LMAX, HD), BF16)
     vector = jax.ShapeDtypeStruct((ROWS,), F32)
-    y, k_new, v_new, stats = pl.pallas_call(
+    y, k_all, v_all, stats = pl.pallas_call(
         step_kernel,
-        out_shape=(hidden, new_row, new_row, jax.ShapeDtypeStruct((8, 128), F32)),
+        out_shape=(pltpu.VMEM((ROWS, D), BF16), pltpu.VMEM((ROWS, LMAX, HD), BF16), pltpu.VMEM((ROWS, LMAX, HD), BF16),
+                   pltpu.VMEM((8, 128), F32)),
         in_specs=[HB] * 20,
-        out_specs=(HB, HB, HB, VM),
+        out_specs=(VM,) * 4,
         scratch_shapes=[
             pltpu.VMEM((SLOTS, CHUNK, D), BF16),
             pltpu.SMEM((ROWS,), jnp.int32),
@@ -492,8 +453,6 @@
             pltpu.VMEM((GROUP * HD,), BF16),
             pltpu.VMEM((HD,), BF16),
             pltpu.VMEM((HD,), BF16),
-            pltpu.VMEM((ROWS, HD), BF16),
-            pltpu.VMEM((ROWS, HD), BF16),
             pltpu.VMEM((ROWS, GROUP, HD), F32),
             pltpu.VMEM((ROWS, GROUP, LMAX), F32),
             pltpu.VMEM((ROWS, GROUP, HD), F32),
@@ -511,45 +470,29 @@
             pltpu.VMEM((8, 128), F32),
             pltpu.VMEM((NDEV, 8, 128), F32),
             DMA((10,)),
-            DMA((8,)),
-            DMA((16,)),
-            DMA((2 * ROWS,)),
-            DMA((SLOTS + 8,)),
-            DMA((2 * QUARTERS,)),
-            DMA((2, NDEV)),
-            DMA((2, NDEV)),
-            DMA((2, NDEV)),
-            DMA((2, NDEV)),
-            DMA((NDEV,)),
-            DMA((NDEV,)),
-            DMA((NDEV + 2,)),
+            DMA((2,)),
+            DMA((SLOTS,)),
+            DMA((QUARTERS,)),
+            DMA((5,)),
+            DMA((5,)),
         ],
-        compiler_params=pltpu.CompilerParams(collective_id=0, has_side_effects=True, vmem_limit_bytes=VMEM_CAP),
+        compiler_params=pltpu.CompilerParams(collective_id=0, has_side_effects=True, vmem_limit_bytes=STEP_VMEM),
         name='step',
     )(seq_lens, next_tok, tok_hidden, g_attn, g_mlp, g_final, jnp.asarray(rotary_freqs()), b_q, b_k, b_v,
       w_q, w_k, w_v, k_cache, v_cache, w_o, w_gate, w_up, w_down, w_head)
     y_out, k_out, v_out, logp, lse = pl.pallas_call(
         finish_kernel,
         out_shape=(hidden, cache, cache, vector, vector),
-        in_specs=[HB] * 7,
+        in_specs=[VM] * 4,
         out_specs=(HB,) * 5,
         scratch_shapes=[
-            pltpu.SMEM((ROWS,), jnp.int32),
-            pltpu.VMEM((ROWS, D), BF16),
-            pltpu.VMEM((ROWS, HD), BF16),
-            pltpu.VMEM((ROWS, HD), BF16),
-            pltpu.VMEM((8, 128), F32),
             pltpu.VMEM((ROWS,), F32),
             pltpu.VMEM((ROWS,), F32),
-            pltpu.VMEM((ROWS, LMAX, HD), BF16),
-            pltpu.VMEM((ROWS, LMAX, HD), BF16),
-            DMA((2, PARTS)),
-            DMA((2, PARTS)),
-            DMA((8,)),
+            DMA((5,)),
         ],
-        compiler_params=pltpu.CompilerParams(vmem_limit_bytes=VMEM_CAP),
+        compiler_params=pltpu.CompilerParams(vmem_limit_bytes=2**20),
         name='finish',
-    )(seq_lens, y, k_new, v_new, stats, k_cache, v_cache)
+    )(y, k_all, v_all, stats)
     shape = (ROWS, LMAX, 1, HD)
     return y_out, k_out.reshape(shape), v_out.reshape(shape), logp, lse
 

time: 69.8 us -> 65.6 us (0.940)
  Pallas kernels: 68.9 us -> 64.7 us
    pallas_call x1, Pallas kernels: 4.29 us -> 2.09 us  [local_step(): pl.pallas_call(finish_kernel, out_shape=(hidden, cache, cache, vector, ve...]
    pallas_call x1, Pallas kernels: 64.6 us -> 62.6 us  [local_step(): pl.pallas_call(step_kernel, out_shape=(pltpu.VMEM((ROWS, D), BF16), pltpu...]
where the time goes in v4:
time: 65.6 us; the launch traced here: 65.5 us
  Pallas kernels  64.7 us (99%)
  between operations  0.81 us (1%)
    pallas_call x1, Pallas kernels, local_step(): pl.pallas_call(step_kernel, out_shape=(pltpu.VMEM((ROWS, D), BF16), pltpu...  62.6 us
    pallas_call x1, Pallas kernels, local_step(): pl.pallas_call(finish_kernel, out_shape=(hidden, cache, cache, vector, ve...  2.09 us

profile of v4, /device:TPU:0, one launch (start us, length us, event | category | flops | bytes accessed | tf_op | source)
XLA Modules:
  0.0 65.5 jit_solution(1340105541075897365)
XLA Ops:
  0.6 62.6 %step.1 = (bf16[16,4096]{1,0:T(8,128)(2,1)S(1)}, bf16[16,512,128]{2,1,0:T(8,128)(2,1)S(1)}, bf16[16,512,128]{2,1,0:T(8,128)(2,1)S(1)}, f32[8,128]{1,0:T(8,128)S(1)}) custom-call(s32[16]{0:T(128)} %lens_hbm.1, s32[16]{0:T(128)} %tok_hbm.1, bf16[16,4096]{1,0:T(8,128)(2,1)} %x_hbm.1, bf16[4096]{0:T(1024)(128)(2,1)} %ga_hbm.1, bf16[4096]{0:T(1024)(128)(2,1)} %gm_hbm.1, ...), custom_call_target="tpu_custom_call" | custom-call | tf_op jit(solution)/shard_map/step/pallas_call | solution.py:438
  63.3 2.1 %finish.1 = (bf16[16,4096]{1,0:T(8,128)(2,1)}, bf16[16,512,128]{2,1,0:T(8,128)(2,1)}, bf16[16,512,128]{2,1,0:T(8,128)(2,1)}, f32[16]{0:T(128)}, f32[16]{0:T(128)}) custom-call(bf16[16,4096]{1,0:T(8,128)(2,1)S(1)} %get-tuple-element.14.y_ref, bf16[16,512,128]{2,1,0:T(8,128)(2,1)S(1)} %get-tuple-element.15.k_ref, ...), custom_call_target="tpu_custom_call" | custom-call | tf_op jit(solution)/shard_map/finish/pallas_call | solution.py:483

commit v5 on v4

--- a/solution.py
+++ b/solution.py
@@ -31,7 +31,7 @@
 NFULL = VOC // CHUNK
 REST = VOC - NFULL * CHUNK
 PAIRS = NFULL // 2
-QUARTERS = 4
+PIECES = ((0, 2048), (2048, 3072), (3072, 4096))
 STEP_VMEM = 56 * 2**20
 
 NT_DIMS = (((1,), (1,)), ((), ()))
@@ -117,11 +117,10 @@
         slot = head_slot(h)
         return copy(wh_hbm.at[pl.ds(pl.multiple_of(head_row(h), 32), CHUNK), :], ring.at[slot], ring_sems.at[slot])
 
-    def head_quarters(h):
+    def head_pieces(h):
         slot = (h + HEAD0) % SLOTS
-        size = D // QUARTERS
-        return [copy(wh_hbm.at[pl.ds(head_row(h), CHUNK), q * size:(q + 1) * size], ring.at[slot, :, q * size:(q + 1) * size],
-                     last_sems.at[q]) for q in range(QUARTERS)]
+        return [copy(wh_hbm.at[pl.ds(head_row(h), CHUNK), lo:hi], ring.at[slot, :, lo:hi], last_sems.at[q])
+                for q, (lo, hi) in enumerate(PIECES)]
 
     def start_chunk(c):
         if c < HEAD0:
@@ -353,19 +352,19 @@
 
         @pl.when(h + SLOTS == 2 * PAIRS)
         def _():
-            for q in range(QUARTERS):
-                for cp in (last_a[q], last_b[q]):
+            for pieces in zip(last_a, last_b):
+                for cp in pieces:
                     cp.start(priority=1)
         return carry
 
-    last_a, last_b = head_quarters(2 * PAIRS), head_quarters(2 * PAIRS + 1)
+    last_a, last_b = head_pieces(2 * PAIRS), head_pieces(2 * PAIRS + 1)
     carry = pair(1, carry, True)
     carry = lax.fori_loop(2, PAIRS, pair, carry)
     sums = zeros(CHUNK)
-    size = D // QUARTERS
-    for q in range(QUARTERS):
-        copy(wo_hbm.at[:, 0:2 * size], ring.at[0, :, 0:2 * size], last_sems.at[q]).wait()
-        sums = score((2 * PAIRS + HEAD0) % SLOTS, (2 * PAIRS + 1 + HEAD0) % SLOTS, CHUNK, q * size, (q + 1) * size, sums)
+    for q, (lo, hi) in enumerate(PIECES):
+        width = 2 * (hi - lo)
+        copy(wo_hbm.at[:, 0:width], ring.at[0, :, 0:width], last_sems.at[q]).wait()
+        sums = score((2 * PAIRS + HEAD0) % SLOTS, (2 * PAIRS + 1 + HEAD0) % SLOTS, CHUNK, lo, hi, sums)
         if q == 0:
             carry = stats((PAIRS - 1) % 2, 2 * PAIRS - 2, carry)
     ca, cb = carry
@@ -472,7 +471,7 @@
             DMA((10,)),
             DMA((2,)),
             DMA((SLOTS,)),
-            DMA((QUARTERS,)),
+            DMA((len(PIECES),)),
             DMA((5,)),
             DMA((5,)),
         ],

time: 65.6 us -> 65.5 us (level)
  no operation moved by 1% of the time
where the time goes in v5:
time: 65.5 us; the launch traced here: 65.4 us
  Pallas kernels  64.6 us (99%)
  between operations  0.81 us (1%)
    pallas_call x1, Pallas kernels, local_step(): pl.pallas_call(step_kernel, out_shape=(pltpu.VMEM((ROWS, D), BF16), pltpu...  62.5 us
    pallas_call x1, Pallas kernels, local_step(): pl.pallas_call(finish_kernel, out_shape=(hidden, cache, cache, vector, ve...  2.09 us

profile of v5, /device:TPU:0, one launch (start us, length us, event | category | flops | bytes accessed | tf_op | source)
XLA Modules:
  0.0 65.4 jit_solution(8087962037808063722)
XLA Ops:
  0.6 62.5 %step.1 = (bf16[16,4096]{1,0:T(8,128)(2,1)S(1)}, bf16[16,512,128]{2,1,0:T(8,128)(2,1)S(1)}, bf16[16,512,128]{2,1,0:T(8,128)(2,1)S(1)}, f32[8,128]{1,0:T(8,128)S(1)}) custom-call(s32[16]{0:T(128)} %lens_hbm.1, s32[16]{0:T(128)} %tok_hbm.1, bf16[16,4096]{1,0:T(8,128)(2,1)} %x_hbm.1, bf16[4096]{0:T(1024)(128)(2,1)} %ga_hbm.1, bf16[4096]{0:T(1024)(128)(2,1)} %gm_hbm.1, ...), custom_call_target="tpu_custom_call" | custom-call | tf_op jit(solution)/shard_map/step/pallas_call | solution.py:437
  63.2 2.1 %finish.1 = (bf16[16,4096]{1,0:T(8,128)(2,1)}, bf16[16,512,128]{2,1,0:T(8,128)(2,1)}, bf16[16,512,128]{2,1,0:T(8,128)(2,1)}, f32[16]{0:T(128)}, f32[16]{0:T(128)}) custom-call(bf16[16,4096]{1,0:T(8,128)(2,1)S(1)} %get-tuple-element.14.y_ref, bf16[16,512,128]{2,1,0:T(8,128)(2,1)S(1)} %get-tuple-element.15.k_ref, ...), custom_call_target="tpu_custom_call" | custom-call | tf_op jit(solution)/shard_map/finish/pallas_call | solution.py:482

commit v6 on v5

--- a/solution.py
+++ b/solution.py
@@ -21,7 +21,7 @@
 VOC = 16032
 COL = 512
 NDEV = 8
-SLOTS = 12
+SLOTS = 10
 CHUNK = 512
 DEEP = 256
 WO = 2
@@ -32,7 +32,7 @@
 REST = VOC - NFULL * CHUNK
 PAIRS = NFULL // 2
 PIECES = ((0, 2048), (2048, 3072), (3072, 4096))
-STEP_VMEM = 56 * 2**20
+STEP_VMEM = 50 * 2**20
 
 NT_DIMS = (((1,), (1,)), ((), ()))
 NN_DIMS = (((1,), (0,)), ((), ()))
@@ -75,7 +75,7 @@
                 ring, lens_ref, tok_ref, x_buf, ga_ref, gm_ref, gf_ref, freq_ref, bq_ref, bk_ref, bv_ref,
                 q_scr, s_scr, o_scr, obuf,
                 mbuf, gacc, uacc, hbuf, za_buf, zb_buf, rs_send, rs_recv, own, gath, st_send, st_recv,
-                small_sems, cache_sems, ring_sems, last_sems, send_sems, recv_sems):
+                small_sems, cache_sems, ring_sems, send_sems, recv_sems):
     me = lax.axis_index('tp')
     peers = {k: flip(me, k) for k in range(1, NDEV)}
     order = (7, 6, 5, 4, 3, 2, 1)
@@ -119,7 +119,7 @@
 
     def head_pieces(h):
         slot = (h + HEAD0) % SLOTS
-        return [copy(wh_hbm.at[pl.ds(head_row(h), CHUNK), lo:hi], ring.at[slot, :, lo:hi], last_sems.at[q])
+        return [copy(wh_hbm.at[pl.ds(head_row(h), CHUNK), lo:hi], ring.at[slot, :, lo:hi], small_sems.at[q])
                 for q, (lo, hi) in enumerate(PIECES)]
 
     def start_chunk(c):
@@ -201,8 +201,8 @@
 
     def exchange(phase, payload, landing, size):
         for k in order:
-            remote(payload(k), landing(k), send_sems.at[phase], recv_sems.at[phase], k).start()
-        return remote(size, size, send_sems.at[phase], recv_sems.at[phase], 1)
+            remote(payload(k), landing(k), send_sems.at[phase % 2], recv_sems.at[phase], k).start()
+        return remote(size, size, send_sems.at[phase % 2], recv_sems.at[phase], 1)
 
     def all_reduce(phase, partial, residual, used, meanwhile):
         def send_part(k):
@@ -265,7 +265,9 @@
             total = total + mm(hbuf[:, first:first + size], ring[(DN0 + j) % SLOTS, 0:size, columns(dev)])
         return total
 
-    sends += all_reduce(1, down, own[0], range(DN0, HEAD0), lambda: None)
+    for group in sends:
+        group.wait_send()
+    sends = all_reduce(1, down, own[0], range(DN0, HEAD0), lambda: None)
     for j in range(NDEV):
         y_ref[:, j * COL:(j + 1) * COL] = gath[1, j]
     norm_cols(gath.at[1], gf_ref[...].astype(F32)[None, :], mbuf)
@@ -363,7 +365,7 @@
     sums = zeros(CHUNK)
     for q, (lo, hi) in enumerate(PIECES):
         width = 2 * (hi - lo)
-        copy(wo_hbm.at[:, 0:width], ring.at[0, :, 0:width], last_sems.at[q]).wait()
+        copy(wo_hbm.at[:, 0:width], ring.at[0, :, 0:width], small_sems.at[q]).wait()
         sums = score((2 * PAIRS + HEAD0) % SLOTS, (2 * PAIRS + 1 + HEAD0) % SLOTS, CHUNK, lo, hi, sums)
         if q == 0:
             carry = stats((PAIRS - 1) % 2, 2 * PAIRS - 2, carry)
@@ -390,6 +392,8 @@
     st_send[0:1, 0:ROWS] = top
     st_send[1:2, 0:ROWS] = acc
     st_send[2:3, 0:ROWS] = hit
+    for group in sends:
+        group.wait_send()
     share = exchange(4, lambda k: st_send, lambda k: st_recv.at[k], st_recv.at[1:NDEV])
     share.wait_recv()
     tops, accs, hits = [top], [acc], [hit]
@@ -402,8 +406,7 @@
     lse = best + jnp.log(exp_sum)
     st_ref[0:1, 0:ROWS] = sum(hits) - lse
     st_ref[1:2, 0:ROWS] = lse
-    for group in sends + [share]:
-        group.wait_send()
+    share.wait_send()
 
 
 def finish_kernel(y_ref, k_ref, v_ref, st_ref, y_hbm, k_hbm, v_hbm, logp_hbm, lse_hbm, logp_ref, lse_ref, sems):
@@ -471,8 +474,7 @@
             DMA((10,)),
             DMA((2,)),
             DMA((SLOTS,)),
-            DMA((len(PIECES),)),
-            DMA((5,)),
+            DMA((2,)),
             DMA((5,)),
         ],
         compiler_params=pltpu.CompilerParams(collective_id=0, has_side_effects=True, vmem_limit_bytes=STEP_VMEM),

time: 65.5 us -> 65.4 us (level)
  no operation moved by 1% of the time
where the time goes in v6:
time: 65.4 us
  Pallas kernels  64.5 us (99%)
  between operations  0.81 us (1%)
    pallas_call x1, Pallas kernels, local_step(): pl.pallas_call(step_kernel, out_shape=(pltpu.VMEM((ROWS, D), BF16), pltpu...  62.5 us
    pallas_call x1, Pallas kernels, local_step(): pl.pallas_call(finish_kernel, out_shape=(hidden, cache, cache, vector, ve...  2.09 us

profile of v6, /device:TPU:0, one launch (start us, length us, event | category | flops | bytes accessed | tf_op | source)
XLA Modules:
  0.0 65.4 jit_solution(10847057833638450582)
XLA Ops:
  0.6 62.5 %step.1 = (bf16[16,4096]{1,0:T(8,128)(2,1)S(1)}, bf16[16,512,128]{2,1,0:T(8,128)(2,1)S(1)}, bf16[16,512,128]{2,1,0:T(8,128)(2,1)S(1)}, f32[8,128]{1,0:T(8,128)S(1)}) custom-call(s32[16]{0:T(128)} %lens_hbm.1, s32[16]{0:T(128)} %tok_hbm.1, bf16[16,4096]{1,0:T(8,128)(2,1)} %x_hbm.1, bf16[4096]{0:T(1024)(128)(2,1)} %ga_hbm.1, bf16[4096]{0:T(1024)(128)(2,1)} %gm_hbm.1, ...), custom_call_target="tpu_custom_call" | custom-call | tf_op jit(solution)/shard_map/step/pallas_call | solution.py:440
  63.1 2.1 %finish.1 = (bf16[16,4096]{1,0:T(8,128)(2,1)}, bf16[16,512,128]{2,1,0:T(8,128)(2,1)}, bf16[16,512,128]{2,1,0:T(8,128)(2,1)}, f32[16]{0:T(128)}, f32[16]{0:T(128)}) custom-call(bf16[16,4096]{1,0:T(8,128)(2,1)S(1)} %get-tuple-element.14.y_ref, bf16[16,512,128]{2,1,0:T(8,128)(2,1)S(1)} %get-tuple-element.15.k_ref, ...), custom_call_target="tpu_custom_call" | custom-call | tf_op jit(solution)/shard_map/finish/pallas_call | solution.py:484
